TPU v7x, 16 devices: a whole 2x2x2 slice. The times are simulated.
16 devices in a mesh: tp: 2 (over z), fsdp: 8 (over y, x, core).
Axes of the slice: x: 2, y: 2, z: 2, core: 2. Of those that a mesh axis runs over, the one named last changes fastest.
Arguments:
- x_in: bfloat16 [128, 256, 2048], P('fsdp')
- grad_y: bfloat16 [128, 256, 2048], P('fsdp')
- w_query: bfloat16 [2048, 2048], P('fsdp', 'tp')
- w_key: bfloat16 [2048, 2048], P('fsdp', 'tp')
- w_value: bfloat16 [2048, 2048], P('fsdp', 'tp')
- w_out: bfloat16 [2048, 2048], P('tp', 'fsdp')
- w_up: bfloat16 [2048, 8192], P('fsdp', 'tp')
- b_up: float32 [8192], P('tp')
- w_down: bfloat16 [8192, 2048], P('tp', 'fsdp')
- ln_scale: float32 [2048], replicated
- q_scale: float32 [256], replicated
- k_scale: float32 [256], replicated
Outputs:
- output 1: bfloat16 [128, 256, 2048], P('fsdp')
- output 2: float32 [2048, 2048], P('fsdp', 'tp')
- output 3: float32 [2048, 2048], P('fsdp', 'tp')
- output 4: float32 [2048, 2048], P('fsdp', 'tp')
- output 5: float32 [2048, 2048], P('tp', 'fsdp')
- output 6: float32 [2048, 8192], P('fsdp', 'tp')
- output 7: float32 [8192], P('tp')
- output 8: float32 [8192, 2048], P('tp', 'fsdp')
- output 9: float32 [2048], replicated
- output 10: float32 [2048], replicated
- output 11: float32 [256], replicated
- output 12: float32 [256], replicated
All inputs are finite; a program needn't handle non-finite values.
Results may differ from a plain program's by a relative error of at most 0.02.
Values are sent between devices in bfloat16 or wider.
A program may use at most 1 GiB of HBM per device.

v0:
```python
import functools
import jax
import jax.numpy as jnp
from jax import lax
from jax.sharding import PartitionSpec as P

EPS = 1e-6


def scaled_norm(values, scale_vec):
    row_mean = jnp.mean(values, axis=-1, keepdims=True)
    centred = values - row_mean
    row_var = jnp.mean(centred * centred, axis=-1, keepdims=True)
    return centred * lax.rsqrt(row_var + EPS) * scale_vec


def exact_gelu(values):
    return jax.nn.gelu(values, approximate=False)


def solution(mesh):
    act_spec = P('fsdp', None, None)
    row_spec = P('fsdp', 'tp')
    col_spec = P('tp', 'fsdp')
    in_specs = (act_spec, act_spec, row_spec, row_spec, row_spec, col_spec, row_spec, P('tp'), col_spec, P(), P(), P())
    out_specs = (act_spec, row_spec, row_spec, row_spec, col_spec, row_spec, P('tp'), col_spec, P(), P(), P(), P())
    gather_rows = functools.partial(lax.all_gather, axis_name='fsdp', axis=0, tiled=True)
    gather_cols = functools.partial(lax.all_gather, axis_name='fsdp', axis=1, tiled=True)
    scatter_rows = functools.partial(lax.psum_scatter, axis_name='fsdp', scatter_dimension=0, tiled=True)
    scatter_cols = functools.partial(lax.psum_scatter, axis_name='fsdp', scatter_dimension=1, tiled=True)

    def local_step(x_in, grad_y, w_query, w_key, w_value, w_out, w_up, b_up, w_down, ln_scale, q_scale, k_scale):
        bf16 = jnp.bfloat16
        fp32 = jnp.float32
        wq_full = gather_rows(w_query)
        wk_full = gather_rows(w_key)
        wv_full = gather_rows(w_value)
        wo_full = gather_cols(w_out)
        wu_full = gather_rows(w_up)
        wd_full = gather_cols(w_down)
        head_dim = q_scale.shape[0]
        num_img = x_in.shape[0]
        num_tok = x_in.shape[1]
        num_heads = wq_full.shape[1] // head_dim
        score_scale = head_dim ** -0.5

        normed_f, ln_pull = jax.vjp(scaled_norm, x_in.astype(fp32), ln_scale)
        normed = normed_f.astype(bf16)

        def project(weight):
            return jnp.einsum('btd,dn->btn', normed, weight, preferred_element_type=fp32).astype(bf16)

        q_proj = project(wq_full).reshape(num_img, num_tok, num_heads, head_dim)
        k_proj = project(wk_full).reshape(num_img, num_tok, num_heads, head_dim)
        v_proj = project(wv_full).reshape(num_img, num_tok, num_heads, head_dim)
        qn_f, q_pull = jax.vjp(scaled_norm, q_proj.astype(fp32), q_scale)
        kn_f, k_pull = jax.vjp(scaled_norm, k_proj.astype(fp32), k_scale)
        q_norm = qn_f.astype(bf16)
        k_norm = kn_f.astype(bf16)
        logits = jnp.einsum('bqhd,bkhd->bhqk', q_norm, k_norm, preferred_element_type=fp32)
        attn_prob = jax.nn.softmax(logits * score_scale, axis=-1)
        prob_b16 = attn_prob.astype(bf16)
        attn_out = jnp.einsum('bhqk,bkhd->bqhd', prob_b16, v_proj, preferred_element_type=fp32).astype(bf16)
        attn_flat = attn_out.reshape(num_img, num_tok, -1)
        hidden = (jnp.einsum('btd,df->btf', normed, wu_full, preferred_element_type=fp32) + b_up).astype(bf16)
        act_f, gelu_pull = jax.vjp(exact_gelu, hidden.astype(fp32))
        act_out = act_f.astype(bf16)

        d_act = jnp.einsum('btd,fd->btf', grad_y, wd_full, preferred_element_type=fp32).astype(bf16)
        d_hidden = gelu_pull(d_act.astype(fp32))[0].astype(bf16)
        grad_w_down = jnp.einsum('btf,btd->fd', act_out, grad_y, preferred_element_type=fp32)
        grad_w_up = jnp.einsum('btd,btf->df', normed, d_hidden, preferred_element_type=fp32)
        grad_b_up = jnp.sum(d_hidden, axis=(0, 1), dtype=fp32)
        d_normed = jnp.einsum('btf,df->btd', d_hidden, wu_full, preferred_element_type=fp32)

        d_attn = jnp.einsum('btd,nd->btn', grad_y, wo_full, preferred_element_type=fp32).astype(bf16)
        grad_w_out = jnp.einsum('btn,btd->nd', attn_flat, grad_y, preferred_element_type=fp32)
        d_attn_heads = d_attn.reshape(num_img, num_tok, num_heads, head_dim)
        d_prob = jnp.einsum('bqhd,bkhd->bhqk', d_attn_heads, v_proj, preferred_element_type=fp32).astype(bf16).astype(fp32)
        d_value = jnp.einsum('bhqk,bqhd->bkhd', prob_b16, d_attn_heads, preferred_element_type=fp32).astype(bf16)
        d_logit = (attn_prob * (d_prob - jnp.sum(attn_prob * d_prob, axis=-1, keepdims=True)) * score_scale).astype(bf16)
        d_qnorm = jnp.einsum('bhqk,bkhd->bqhd', d_logit, k_norm, preferred_element_type=fp32).astype(bf16)
        d_knorm = jnp.einsum('bhqk,bqhd->bkhd', d_logit, q_norm, preferred_element_type=fp32).astype(bf16)
        d_query_f, grad_q_scale = q_pull(d_qnorm.astype(fp32))
        d_key_f, grad_k_scale = k_pull(d_knorm.astype(fp32))
        d_query = d_query_f.astype(bf16).reshape(num_img, num_tok, -1)
        d_key = d_key_f.astype(bf16).reshape(num_img, num_tok, -1)
        d_value_flat = d_value.reshape(num_img, num_tok, -1)
        grad_w_query = jnp.einsum('btd,btn->dn', normed, d_query, preferred_element_type=fp32)
        grad_w_key = jnp.einsum('btd,btn->dn', normed, d_key, preferred_element_type=fp32)
        grad_w_value = jnp.einsum('btd,btn->dn', normed, d_value_flat, preferred_element_type=fp32)
        d_normed = (d_normed
                    + jnp.einsum('btn,dn->btd', d_query, wq_full, preferred_element_type=fp32)
                    + jnp.einsum('btn,dn->btd', d_key, wk_full, preferred_element_type=fp32)
                    + jnp.einsum('btn,dn->btd', d_value_flat, wv_full, preferred_element_type=fp32))
        d_normed = lax.psum(d_normed, 'tp')
        d_x_f, grad_ln_scale = ln_pull(d_normed.astype(bf16).astype(fp32))
        grad_x = (grad_y.astype(fp32) + d_x_f).astype(bf16)
        grad_b_down = jnp.sum(grad_y, axis=(0, 1), dtype=fp32)
        return (grad_x, scatter_rows(grad_w_query), scatter_rows(grad_w_key), scatter_rows(grad_w_value),
                scatter_cols(grad_w_out), scatter_rows(grad_w_up), lax.psum(grad_b_up, 'fsdp'),
                scatter_cols(grad_w_down), lax.psum(grad_b_down, 'fsdp'), lax.psum(grad_ln_scale, 'fsdp'),
                lax.psum(grad_q_scale, ('tp', 'fsdp')), lax.psum(grad_k_scale, ('tp', 'fsdp')))

    return jax.shard_map(local_step, mesh=mesh, in_specs=in_specs, out_specs=out_specs, check_vma=False)
```

profile of v0, /device:TPU:0, one launch (start us, length us, event | category | flops | bytes accessed | tf_op | source)
XLA Modules:
  0.0 2202.7 jit_solution(11507630812058202441)
XLA Ops:
  45.5 23.8 %convert_convert_fusion = f32[16,256,1024]{2,1,0:T(8,128)} fusion(bf16[2048,1024]{1,0:T(8,128)(2,1)} %all-gather.13.cloned.1.call-done, bf16[16,256,2048]{2,1,0:T(8,128)(2,1)} %param.12, f32[2048]{0:T(1024)S(1)} %copy-done.19, f32[16,256]{1,0:T(8,128)S(1)} %fusion.103, f32[16,256]{1,0:T(8,128)S(1)} %broadcast_multiply_fusion.2), kind=kOutput, calls=%fused_computation.107 | convolution fusion | flops 17230200832 | bytes 37789696 | tf_op jit(solution)/shard_map/btd,dn->btn/dot_general | solution.py:51
  120.0 24.2 %convert_convert_fusion.1 = f32[16,256,1024]{2,1,0:T(8,128)} fusion(bf16[2048,1024]{1,0:T(8,128)(2,1)} %all-gather.11.cloned.1.call-done, bf16[16,256,2048]{2,1,0:T(8,128)(2,1)} %param.12, f32[2048]{0:T(1024)S(1)} %copy-done.19, f32[16,256]{1,0:T(8,128)S(1)} %fusion.103, f32[16,256]{1,0:T(8,128)S(1)} %broadcast_multiply_fusion.2), kind=kOutput, calls=%fused_computation.108 | convolution fusion | flops 17230200832 | bytes 37789696 | tf_op jit(solution)/shard_map/btd,dn->btn/dot_general | solution.py:51
  194.4 37.1 %convolution_convert_fusion.3 = bf16[16,256,1024]{2,1,0:T(8,128)(2,1)} fusion(bf16[2048,1024]{1,0:T(8,128)(2,1)} %all-gather.17.cloned.1.call-done, bf16[16,256,2048]{2,1,0:T(8,128)(2,1)} %param.12, f32[2048]{0:T(1024)S(1)} %copy-done.19, f32[16,256]{1,0:T(8,128)S(1)} %fusion.103, f32[16,256]{1,0:T(8,128)S(1)} %broadcast_multiply_fusion.2), kind=kOutput, calls=%fused_computation.114 | convolution fusion | flops 17226006528 | bytes 29401088 | tf_op jit(solution)/shard_map/btd,dn->btn/dot_general | solution.py:51
  266.2 20.8 fusion.110
  319.0 23.9 %convolution_bitcast_fusion.1 = f32[1024,2048]{1,0:T(8,128)} fusion(bf16[16,256,1024]{1,2,0:T(8,128)(2,1)} %bitcast.121, bf16[16,256,2048]{2,1,0:T(8,128)(2,1)} %param.13), kind=kOutput, calls=%fused_computation.116 | convolution fusion | flops 17179869184 | bytes 33554432 | tf_op jit(solution)/shard_map/btn,btd->nd/dot_general | solution.py:77
  343.0 24.2 %convolution_convert_fusion.4 = bf16[16,256,1024]{2,1,0:T(8,128)(2,1)} fusion(bf16[16,256,2048]{2,1,0:T(8,128)(2,1)} %param.13, bf16[1024,2048]{1,0:T(8,128)(2,1)} %all-gather.15.cloned.1.call-done), kind=kOutput, calls=%fused_computation.115 | convolution fusion | flops 17184063488 | bytes 29360128 | tf_op jit(solution)/shard_map/btd,nd->btn/dot_general | solution.py:76
  391.3 32.8 %fusion.67 = (f32[16,256,4]{1,2,0:T(4,128)S(1)}, bf16[16,4,256,256]{3,2,1,0:T(8,128)(2,1)}) fusion(f32[16,256,4,256]{1,3,2,0:T(8,128)} %copy.126, f32[256]{0:T(256)S(1)} %copy-done.23, f32[16,256,4]{1,2,0:T(4,128)S(1)} %copy.125, bf16[16,4,256,256]{2,3,1,0:T(8,128)(2,1)} %convolution_convert_fusion.2, f32[16,4,256,256]{2,3,1,0:T(8,128)} %get-tuple-element.26, ...), kind=kOutput, calls=%fused_computation.88 | convolution fusion | flops 2227175680 | bytes 67438592 | tf_op jit(solution)/shard_map/bhqk,bkhd->bqhd/dot_general | solution.py:82
  437.0 27.7 %convolution_bitcast_fusion.2 = f32[2048,1024]{1,0:T(8,128)} fusion(bf16[16,256,1024]{1,2,0:T(8,128)(2,1)} %bitcast.117, bf16[16,256,2048]{2,1,0:T(8,128)(2,1)} %param.12, f32[2048]{0:T(1024)S(1)} %copy-done.20, f32[16,256]{1,0:T(8,128)S(1)} %copy-done.14, f32[16,256]{1,0:T(8,128)S(1)} %copy-done.10), kind=kOutput, calls=%fused_computation.117 | convolution fusion | flops 17221812224 | bytes 33595392 | tf_op jit(solution)/shard_map/btd,btn->dn/dot_general | solution.py:91
  464.8 36.4 %fusion.63 = (f32[16,256,4]{1,2,0:T(4,128)S(1)}, bf16[16,4,256,256]{3,2,1,0:T(8,128)(2,1)}) fusion(f32[16,256,4,256]{1,3,2,0:T(8,128)} %copy.121, f32[256]{0:T(256)S(1)} %copy-done.24, f32[16,256,4]{1,2,0:T(4,128)S(1)} %copy.120, bf16[16,4,256,256]{2,3,1,0:T(8,128)(2,1)} %convolution_convert_fusion.2, f32[16,4,256,256]{2,3,1,0:T(8,128)} %get-tuple-element.26, ...), kind=kOutput, calls=%fused_computation.82 | convolution fusion | flops 2227175680 | bytes 67438592 | tf_op jit(solution)/shard_map/bhqk,bqhd->bkhd/dot_general | solution.py:83
  501.3 30.1 %fusion.64 = (f32[256]{0:T(256)}, f32[16,256,4]{1,2,0:T(4,128)S(1)}, f32[16,256,4]{1,2,0:T(4,128)S(1)}, f32[256]{0:T(256)}) fusion(bf16[16,4,256,256]{3,2,1,0:T(8,128)(2,1)} %get-tuple-element.28, f32[16,256,4,256]{1,3,2,0:T(8,128)} %copy.121, f32[16,256,4]{1,2,0:T(4,128)S(1)} %copy.123, f32[16,256,4]{1,2,0:T(4,128)S(1)} %copy.120, ...), kind=kLoop, calls=%fused_computation.83 | loop fusion | flops 92241408 | bytes 50860032 | tf_op jit(solution)/shard_map/transpose(jvp())/reduce_sum | solution.py:14
  544.6 28.1 %convolution_bitcast_fusion.4 = f32[2048,1024]{1,0:T(8,128)} fusion(bf16[16,256,1024]{1,2,0:T(8,128)(2,1)} %bitcast.113, bf16[16,256,2048]{2,1,0:T(8,128)(2,1)} %param.12, f32[2048]{0:T(1024)S(1)} %copy-done.20, f32[16,256]{1,0:T(8,128)S(1)} %copy-done.14, f32[16,256]{1,0:T(8,128)S(1)} %copy-done.10), kind=kOutput, calls=%fused_computation.119 | convolution fusion | flops 17221812224 | bytes 33595392 | tf_op jit(solution)/shard_map/btd,btn->dn/dot_general | solution.py:89
  602.9 28.1 %convolution_bitcast_fusion.3 = f32[2048,1024]{1,0:T(8,128)} fusion(bf16[16,256,1024]{1,2,0:T(8,128)(2,1)} %bitcast.115, bf16[16,256,2048]{2,1,0:T(8,128)(2,1)} %param.12, f32[2048]{0:T(1024)S(1)} %copy-done.20, f32[16,256]{1,0:T(8,128)S(1)} %copy-done.14, f32[16,256]{1,0:T(8,128)S(1)} %copy-done.10), kind=kOutput, calls=%fused_computation.118 | convolution fusion | flops 17221812224 | bytes 33595392 | tf_op jit(solution)/shard_map/btd,btn->dn/dot_general | solution.py:90
  631.1 234.5 %fusion.32 = (f32[16,256,4096]{2,1,0:T(8,128)}, bf16[16,256,4096]{2,1,0:T(8,128)(2,1)}) fusion(f32[4096]{0:T(1024)S(1)} %copy-done.30, bf16[2048,4096]{1,0:T(8,128)(2,1)} %all-gather.7.cloned.1.call-done, bf16[16,256,2048]{2,1,0:T(8,128)(2,1)} %fusion.118.clone.4), kind=kOutput, calls=%fused_computation.37 | convolution fusion | flops 69809995776 | bytes 134234112 | tf_op jit(solution)/shard_map/btd,df->btf/dot_general | solution.py:65
  865.6 84.0 %fusion.55 = f32[4096,2048]{1,0:T(8,128)} fusion(bf16[16,256,2048]{2,1,0:T(8,128)(2,1)} %param.13, f32[16,256,4096]{2,1,0:T(8,128)} %get-tuple-element.31, bf16[16,256,4096]{2,1,0:T(8,128)(2,1)} %get-tuple-element.32), kind=kOutput, calls=%fused_computation.73 | convolution fusion | flops 68786585600 | bytes 150994944 | tf_op jit(solution)/shard_map/btf,btd->fd/dot_general | solution.py:71
  950.3 34.3 %all-reduce = (f32[256]{0:T(256)}, f32[256]{0:T(256)}) all-reduce(f32[256]{0:T(256)S(1)} %copy-done.27, f32[256]{0:T(256)S(1)} %copy-done.26), channel_id=1, replica_groups=mesh['tp'=2,'fsdp'=8] {'tp','fsdp'}, use_global_device_ids=true, to_apply=%region_29.0 | all-reduce | flops 512 | bytes 4096 | tf_op jit(solution)/shard_map/psum | solution.py:103
  984.6 27.2 %fusion.88 = f32[16,256,2048]{2,1,0:T(8,128)} fusion(bf16[16,256,1024]{1,2,0:T(8,128)(2,1)} %bitcast.116, bf16[2048,1024]{1,0:T(8,128)(2,1)} %all-gather.11.cloned.1.call-done), kind=kOutput, calls=%fused_computation.127 | convolution fusion | flops 17179869184 | bytes 46137344 | tf_op jit(solution)/shard_map/btn,dn->btd/dot_general | solution.py:94
  1011.9 23.2 %fusion.85 = f32[16,256,2048]{2,1,0:T(8,128)} fusion(bf16[16,256,1024]{1,2,0:T(8,128)(2,1)} %bitcast.114, bf16[2048,1024]{1,0:T(8,128)(2,1)S(1)} %copy-done.28), kind=kOutput, calls=%fused_computation.124 | convolution fusion | flops 17179869184 | bytes 46137344 | tf_op jit(solution)/shard_map/btn,dn->btd/dot_general | solution.py:93
  1035.1 21.8 fusion.81
  1056.9 112.1 %convert_reduce_fusion = (f32[4096]{0:T(1024)}, bf16[16,256,4096]{2,1,0:T(8,128)(2,1)}) fusion(f32[16,256,4096]{2,1,0:T(8,128)} %get-tuple-element.31, bf16[16,256,2048]{2,1,0:T(8,128)(2,1)} %param.13, bf16[4096,2048]{1,0:T(8,128)(2,1)} %all-gather.9.cloned.1.call-done, bf16[16,256,4096]{2,1,0:T(8,128)(2,1)} %get-tuple-element.32), kind=kOutput, calls=%fused_computation.45 | convolution fusion | flops 69038243840 | bytes 167788544 | tf_op jit(solution)/shard_map/btd,fd->btf/dot_general | solution.py:69
  1169.0 83.8 %convolution_bitcast_fusion = f32[2048,4096]{1,0:T(8,128)} fusion(bf16[16,256,4096]{2,1,0:T(8,128)(2,1)} %get-tuple-element.34, bf16[16,256,2048]{2,1,0:T(8,128)(2,1)} %param.12, f32[2048]{0:T(1024)S(1)} %copy-done.21, f32[16,256]{1,0:T(8,128)S(1)} %copy-done.15, f32[16,256]{1,0:T(8,128)S(1)} %copy-done.11), kind=kOutput, calls=%fused_computation.74 | convolution fusion | flops 68761419776 | bytes 83927040 | tf_op jit(solution)/shard_map/btd,btf->df/dot_general | solution.py:72
  1252.9 96.4 %add_add_fusion.1 = f32[16,256,2048]{2,1,0:T(8,128)} fusion(f32[16,256,2048]{2,1,0:T(8,128)} %fusion.81, f32[16,256,2048]{2,1,0:T(8,128)} %fusion.88, f32[16,256,2048]{2,1,0:T(8,128)} %fusion.85, bf16[16,256,4096]{2,1,0:T(8,128)(2,1)} %get-tuple-element.34, bf16[2048,4096]{1,0:T(8,128)(2,1)} %all-gather.7.cloned.1.call-done), kind=kOutput, calls=%fused_computation.66 | convolution fusion | flops 68744642560 | bytes 184549376 | tf_op jit(solution)/shard_map/btf,df->btd/dot_general | solution.py:74
  1349.3 756.7 %all-reduce.3 = bf16[16,256,2048]{2,1,0:T(8,128)(2,1)} all-reduce(f32[16,256,2048]{2,1,0:T(8,128)} %add_add_fusion.1), channel_id=1, replica_groups=mesh['tp'=2,'fsdp'=8] {'tp'}, use_global_device_ids=true, to_apply=%region_13.0 | all-reduce | flops 8388608 | bytes 50331648 | tf_op jit(solution)/shard_map/psum | solution.py:96
  2144.0 28.7 %convert_reduce_fusion.2 = (f32[2048]{0:T(1024)S(1)}, bf16[16,256,2048]{2,1,0:T(8,128)(2,1)}) fusion(bf16[16,256,2048]{2,1,0:T(8,128)(2,1)} %param.13, f32[16,256]{1,0:T(8,128)S(1)} %negate_multiply_fusion, f32[16,256]{1,0:T(8,128)S(1)} %multiply_multiply_fusion, f32[16,256]{1,0:T(8,128)S(1)} %copy-done.12, bf16[16,256,2048]{2,1,0:T(8,128)(2,1)} %param.12, ...), kind=kLoop, calls=%fused_computation.56 | loop fusion | flops 109049856 | bytes 67190784 | tf_op jit(solution)/shard_map/reduce_sum | solution.py:99
  2172.7 23.0 %all-reduce.1 = (f32[4096]{0:T(1024)}, f32[2048]{0:T(1024)}, f32[2048]{0:T(1024)}) all-reduce(f32[4096]{0:T(1024)S(1)} %copy-done.25, f32[2048]{0:T(1024)S(1)} %get-tuple-element.23, f32[2048]{0:T(1024)S(1)} %get-tuple-element.12), channel_id=1, replica_groups=mesh['tp'=2,'fsdp'=8] {'fsdp'}, use_global_device_ids=true, to_apply=%region_22.0 | all-reduce | flops 8192 | bytes 65536 | tf_op jit(solution)/shard_map/psum | solution.py:101
  (146 shorter events, 324.9 us)
Async XLA Ops:
  7.2 38.3 %all-gather.13.cloned.1.call-start = ((), (), s32[]{:S(2)}) async-start(), calls=%async_computation.9 | async-start | bytes 4718592 | tf_op jit(solution)/shard_map/all_gather | solution.py:35
  7.9 112.1 %all-gather.11.cloned.1.call-start = ((), (), s32[]{:S(2)}) async-start(), calls=%async_computation.8 | async-start | bytes 4718592 | tf_op jit(solution)/shard_map/all_gather | solution.py:36
  8.7 185.7 %all-gather.17.cloned.1.call-start = ((), (), s32[]{:S(2)}) async-start(), calls=%async_computation.11 | async-start | bytes 4718592 | tf_op jit(solution)/shard_map/all_gather | solution.py:37
  9.4 333.6 %all-gather.15.cloned.1.call-start = ((), (), s32[]{:S(2)}) async-start(), calls=%async_computation.10 | async-start | bytes 4718592 | tf_op jit(solution)/shard_map/all_gather | solution.py:38
  10.0 621.1 %all-gather.7.cloned.1.call-start = ((), (), s32[]{:S(2)}) async-start(), calls=%async_computation.6 | async-start | bytes 18874368 | tf_op jit(solution)/shard_map/all_gather | solution.py:39
  10.6 1046.3 %all-gather.9.cloned.1.call-start = ((), (), s32[]{:S(2)}) async-start(), calls=%async_computation.7 | async-start | bytes 18874368 | tf_op jit(solution)/shard_map/all_gather | solution.py:40
  11.1 34.4 %copy-start.19 = (f32[2048]{0:T(1024)S(1)}, f32[2048]{0:T(1024)}, u32[]{:S(2)}) copy-start(f32[2048]{0:T(1024)} %param.21) | copy-start | bytes 24580
  11.1 2184.5 %reduce-scatter.13.cloned.1.call-start = ((), (), s32[]{:S(2)}) async-start(), calls=%async_computation.15 | async-start | bytes 9437184 | tf_op jit(solution)/shard_map/reduce_scatter | solution.py:101
  22.4 172.0 %copy-start.9 = (f32[16,256]{1,0:T(8,128)}, f32[16,256]{1,0:T(8,128)S(1)}, u32[]{:S(2)}) copy-start(f32[16,256]{1,0:T(8,128)S(1)} %broadcast_multiply_fusion.2) | copy-start | bytes 49156
  28.5 165.8 %copy-start.13 = (f32[16,256]{1,0:T(8,128)}, f32[16,256]{1,0:T(8,128)S(1)}, u32[]{:S(2)}) copy-start(f32[16,256]{1,0:T(8,128)S(1)} %fusion.103) | copy-start | bytes 49156
  256.5 30.5 %copy-start.3 = (f32[16,256,4]{1,2,0:T(4,128)}, f32[16,256,4]{1,2,0:T(4,128)S(1)}, u32[]{:S(2)}) copy-start(f32[16,256,4]{1,2,0:T(4,128)S(1)} %copy.128) | copy-start | bytes 196612
  342.9 1852.7 %reduce-scatter.11.cloned.1.call-start = ((), (), s32[]{:S(2)}) async-start(), calls=%async_computation.14 | async-start | bytes 9437184 | tf_op jit(solution)/shard_map/reduce_scatter | solution.py:100
  391.3 32.8 %copy-start.8 = (f32[16,256,4]{1,2,0:T(4,128)S(1)}, f32[16,256,4]{1,2,0:T(4,128)}, u32[]{:S(2)}) copy-start(f32[16,256,4]{1,2,0:T(4,128)} %copy-done.7) | copy-start | bytes 196612
  464.7 36.5 %copy-start.6 = (f32[16,256,4]{1,2,0:T(4,128)S(1)}, f32[16,256,4]{1,2,0:T(4,128)}, u32[]{:S(2)}) copy-start(f32[16,256,4]{1,2,0:T(4,128)} %copy-done.5) | copy-start | bytes 196612
  464.7 1731.0 %reduce-scatter.7.cloned.1.call-start = ((), (), s32[]{:S(2)}) async-start(), calls=%async_computation.12 | async-start | bytes 9437184 | tf_op jit(solution)/shard_map/reduce_scatter | solution.py:100
  572.7 1622.9 %reduce-scatter.9.cloned.1.call-start = ((), (), s32[]{:S(2)}) async-start(), calls=%async_computation.13 | async-start | bytes 9437184 | tf_op jit(solution)/shard_map/reduce_scatter | solution.py:100
  631.0 1564.6 %reduce-scatter.17.cloned.1.call-start = ((), (), s32[]{:S(2)}) async-start(), calls=%async_computation.17 | async-start | bytes 37748736 | tf_op jit(solution)/shard_map/reduce_scatter | solution.py:102
  949.7 1246.0 %reduce-scatter.15.cloned.1.call-start = ((), (), s32[]{:S(2)}) async-start(), calls=%async_computation.16 | async-start | bytes 37748736 | tf_op jit(solution)/shard_map/reduce_scatter | solution.py:101
  984.6 50.4 %slice-start = ((s8[8388608]{0:T(1024)(128)(4,1)}), s8[4194304]{0:T(1024)(128)(4,1)S(1)}, s32[]{:S(2)}) async-start(s8[8388608]{0:T(1024)(128)(4,1)} %bitcast.118), calls=%async_computation.18 | async-start | bytes 8388608
  1056.9 112.1 %copy-start.11 = (f32[16,256]{1,0:T(8,128)S(1)}, f32[16,256]{1,0:T(8,128)}, u32[]{:S(2)}) copy-start(f32[16,256]{1,0:T(8,128)} %copy-done.9) | copy-start | bytes 49156
  1056.9 112.1 %copy-start.15 = (f32[16,256]{1,0:T(8,128)S(1)}, f32[16,256]{1,0:T(8,128)}, u32[]{:S(2)}) copy-start(f32[16,256]{1,0:T(8,128)} %copy-done.13) | copy-start | bytes 49156
  1056.9 112.1 %copy-start.21 = (f32[2048]{0:T(1024)S(1)}, f32[2048]{0:T(1024)}, u32[]{:S(2)}) copy-start(f32[2048]{0:T(1024)} %param.21) | copy-start | bytes 24580
  1349.3 756.7 %copy-start.12 = (f32[16,256]{1,0:T(8,128)S(1)}, f32[16,256]{1,0:T(8,128)}, u32[]{:S(2)}) copy-start(f32[16,256]{1,0:T(8,128)} %copy-done.9) | copy-start | bytes 49156
  1349.3 756.7 %copy-start.22 = (f32[2048]{0:T(1024)S(1)}, f32[2048]{0:T(1024)}, u32[]{:S(2)}) copy-start(f32[2048]{0:T(1024)} %param.21) | copy-start | bytes 24580
  (21 other events, 346.4 us)
Sparse Core Ops, SparseCore 0:
  9.8 35.6 all-gather.12
  47.3 32.8 all-gather.10
  82.1 32.8 all-gather.16
  116.6 33.5 all-gather.14
  152.0 85.9 all-gather.6
  239.7 89.2 all-gather.8
  343.1 67.8 reduce-scatter.12
  464.8 67.6 reduce-scatter.10
  572.8 67.7 reduce-scatter.6
  644.5 65.9 reduce-scatter.8
  949.8 202.6 reduce-scatter.16
  1253.0 201.1 reduce-scatter.14
where the time goes:
time: 2210 us; the launch traced here: 2200 us
  matrix products  1030 us (47%)
  blocking collectives  814 us (37%)
  other arithmetic  209 us (9%)
  local copies, waits for them, and re-layouts  116 us (5%)
    psum x1, blocking collectives, local_step(): d_normed = lax.psum(d_normed, 'tp')  757 us
    dot_general x1, matrix products, local_step(): jnp.einsum('btd,df->btf', normed, wu_full, preferred_element_type=fp32)  234 us
    dot_general x1, matrix products, local_step(): jnp.einsum('btd,fd->btf', grad_y, wd_full, preferred_element_type=fp32)  112 us
    dot_general x1, matrix products, local_step(): jnp.einsum('btf,df->btd', d_hidden, wu_full, preferred_element_type=fp32)  96.4 us
    dot_general x3, matrix products, project(): jnp.einsum('btd,dn->btn', normed, weight, preferred_element_type=fp32)  85.1 us
    dot_general x1, matrix products, local_step(): jnp.einsum('btf,btd->fd', act_out, grad_y, preferred_element_type=fp32)  84 us
    dot_general x1, matrix products, local_step(): jnp.einsum('btd,btf->df', normed, d_hidden, preferred_element_type=fp32)  83.8 us
    reduce_sum x3, other arithmetic, scaled_norm(): return centred * lax.rsqrt(row_var + EPS) * scale_vec  64.6 us
  transfers between devices with their start and end apart: 12, of which 1 were waited for; matrix products, arithmetic and copies ran while one was open for 61% of the time, Pallas kernels for 0%

commit v1 on v0

v1 whole, which is shorter than its diff:
```python
import functools
import jax
import jax.numpy as jnp
from jax import lax
from jax.experimental import pallas as pl
from jax.experimental.pallas import tpu as pltpu
from jax.sharding import PartitionSpec as P

EPS = 1e-6
bf16 = jnp.bfloat16
fp32 = jnp.float32
CHUNKS = 4


def dot_nn(a, b):
    return lax.dot_general(a, b, (((1,), (0,)), ((), ())), preferred_element_type=fp32)


def dot_nt(a, b):
    return lax.dot_general(a, b, (((1,), (1,)), ((), ())), preferred_element_type=fp32)


def dot_tn(a, b):
    return lax.dot_general(a, b, (((0,), (0,)), ((), ())), preferred_element_type=fp32)


def norm_parts(values):
    centred = values - jnp.mean(values, axis=-1, keepdims=True)
    inv = lax.rsqrt(jnp.mean(centred * centred, axis=-1, keepdims=True) + EPS)
    return centred * inv, inv


def norm_back(unit, inv, gain, cot):
    d_unit = cot * gain
    m_one = jnp.mean(d_unit, axis=-1, keepdims=True)
    m_two = jnp.mean(d_unit * unit, axis=-1, keepdims=True)
    return inv * (d_unit - m_one - unit * m_two)


def attn_kernel(heads, dim, q_ref, k_ref, v_ref, do_ref, gq_ref, gk_ref, o_ref, dqkv_ref, dgq_ref, dgk_ref):
    @pl.when(pl.program_id(0) == 0)
    def _():
        dgq_ref[...] = jnp.zeros_like(dgq_ref)
        dgk_ref[...] = jnp.zeros_like(dgk_ref)

    scale = dim ** -0.5
    width = heads * dim
    gain_q = gq_ref[...]
    gain_k = gk_ref[...]
    tot_q = jnp.zeros((8, dim), fp32)
    tot_k = jnp.zeros((8, dim), fp32)
    for head in range(heads):
        cols = slice(head * dim, (head + 1) * dim)
        q_unit, q_inv = norm_parts(q_ref[:, cols].astype(fp32))
        k_unit, k_inv = norm_parts(k_ref[:, cols].astype(fp32))
        q_norm = (q_unit * gain_q).astype(bf16)
        k_norm = (k_unit * gain_k).astype(bf16)
        val = v_ref[:, cols]
        d_out = do_ref[:, cols]
        logit_t = dot_nt(k_norm, q_norm) * scale
        expo = jnp.exp(logit_t - jnp.max(logit_t, axis=0, keepdims=True))
        prob_t = expo / jnp.sum(expo, axis=0, keepdims=True)
        prob_b = prob_t.astype(bf16)
        o_ref[:, cols] = dot_tn(prob_b, val).astype(bf16)
        d_prob = dot_nt(val, d_out).astype(bf16).astype(fp32)
        dqkv_ref[:, 2 * width + head * dim:2 * width + (head + 1) * dim] = dot_nn(prob_b, d_out).astype(bf16)
        row = jnp.sum(prob_t * d_prob, axis=0, keepdims=True)
        d_logit = (prob_t * (d_prob - row) * scale).astype(bf16)
        d_qn = dot_tn(d_logit, k_norm).astype(bf16).astype(fp32)
        d_kn = dot_nn(d_logit, q_norm).astype(bf16).astype(fp32)
        dqkv_ref[:, cols] = norm_back(q_unit, q_inv, gain_q, d_qn).astype(bf16)
        dqkv_ref[:, width + head * dim:width + (head + 1) * dim] = norm_back(k_unit, k_inv, gain_k, d_kn).astype(bf16)
        tot_q = tot_q + jnp.sum((d_qn * q_unit).reshape(-1, 8, dim), axis=0)
        tot_k = tot_k + jnp.sum((d_kn * k_unit).reshape(-1, 8, dim), axis=0)
    dgq_ref[...] += tot_q
    dgk_ref[...] += tot_k


def attention(qkv, d_attn, q_scale, k_scale, num_img):
    total, width3 = qkv.shape
    width = width3 // 3
    dim = q_scale.shape[0]
    tok = total // num_img
    heads = width // dim
    part = lambda col: pl.BlockSpec((tok, width), lambda i, col=col: (i, col))
    whole = lambda rows: pl.BlockSpec((rows, dim), lambda i: (0, 0))
    return pl.pallas_call(
        functools.partial(attn_kernel, heads, dim),
        grid=(num_img,),
        in_specs=[part(0), part(1), part(2), part(0), whole(1), whole(1)],
        out_specs=[part(0), pl.BlockSpec((tok, width3), lambda i: (i, 0)), whole(8), whole(8)],
        out_shape=[jax.ShapeDtypeStruct((total, width), bf16), jax.ShapeDtypeStruct((total, width3), bf16),
                   jax.ShapeDtypeStruct((8, dim), fp32), jax.ShapeDtypeStruct((8, dim), fp32)],
        compiler_params=pltpu.CompilerParams(dimension_semantics=("arbitrary",), vmem_limit_bytes=56 * 2 ** 20),
        cost_estimate=pl.CostEstimate(flops=5 * 12 * total * tok * width, bytes_accessed=16 * total * width,
                                      transcendentals=total * tok * heads),
        name="attn",
    )(qkv, qkv, qkv, d_attn, q_scale.reshape(1, dim), k_scale.reshape(1, dim))


def mlp_kernel(sub, h_ref, gy_ref, wu_ref, wd_ref, b_ref, act_ref, dh_ref, db_ref):
    @pl.when(pl.program_id(1) == 0)
    def _():
        db_ref[...] = jnp.zeros_like(db_ref)

    h = h_ref[...]
    gy = gy_ref[...]
    for start in range(0, act_ref.shape[1], sub):
        cols = slice(start, start + sub)
        hid = (dot_nn(h, wu_ref[:, cols]) + b_ref[:, cols]).astype(bf16).astype(fp32)
        d_act = dot_nt(gy, wd_ref[cols, :]).astype(bf16).astype(fp32)
        cdf = 0.5 + 0.5 * lax.erf(hid * (0.5 ** 0.5))
        pdf = jnp.exp(hid * hid * -0.5) * 0.3989422804014327
        act_ref[:, cols] = (hid * cdf).astype(bf16)
        d_hid = (d_act * (cdf + hid * pdf)).astype(bf16)
        dh_ref[:, cols] = d_hid
        db_ref[:, cols] += jnp.sum(d_hid.astype(fp32).reshape(-1, 8, sub), axis=0)


def mlp(normed, grad_y, w_up, w_down, b_up, rows, cols, sub):
    total, depth = normed.shape
    width = w_up.shape[1]
    row_spec = pl.BlockSpec((rows, depth), lambda j, i: (i, 0))
    out_spec = pl.BlockSpec((rows, cols), lambda j, i: (i, j))
    return pl.pallas_call(
        functools.partial(mlp_kernel, sub),
        grid=(width // cols, total // rows),
        in_specs=[row_spec, row_spec, pl.BlockSpec((depth, cols), lambda j, i: (0, j)),
                  pl.BlockSpec((cols, depth), lambda j, i: (j, 0)), pl.BlockSpec((1, cols), lambda j, i: (0, j))],
        out_specs=[out_spec, out_spec, pl.BlockSpec((8, cols), lambda j, i: (0, j))],
        out_shape=[jax.ShapeDtypeStruct((total, width), bf16), jax.ShapeDtypeStruct((total, width), bf16),
                   jax.ShapeDtypeStruct((8, width), fp32)],
        compiler_params=pltpu.CompilerParams(dimension_semantics=("arbitrary", "arbitrary"),
                                             vmem_limit_bytes=60 * 2 ** 20),
        cost_estimate=pl.CostEstimate(flops=4 * total * depth * width, bytes_accessed=16 * total * width,
                                      transcendentals=2 * total * width),
        name="mlp",
    )(normed, grad_y, w_up, w_down, b_up.reshape(1, width))


def after(value, *earlier):
    return lax.optimization_barrier((value,) + earlier)[0]


def solution(mesh):
    act_spec = P('fsdp', None, None)
    row_spec = P('fsdp', 'tp')
    col_spec = P('tp', 'fsdp')
    in_specs = (act_spec, act_spec, row_spec, row_spec, row_spec, col_spec, row_spec, P('tp'), col_spec, P(), P(), P())
    out_specs = (act_spec, row_spec, row_spec, row_spec, col_spec, row_spec, P('tp'), col_spec, P(), P(), P(), P())
    gather_rows = functools.partial(lax.all_gather, axis_name='fsdp', axis=0, tiled=True)
    gather_cols = functools.partial(lax.all_gather, axis_name='fsdp', axis=1, tiled=True)
    scatter_rows = functools.partial(lax.psum_scatter, axis_name='fsdp', scatter_dimension=0, tiled=True)
    scatter_cols = functools.partial(lax.psum_scatter, axis_name='fsdp', scatter_dimension=1, tiled=True)
    num_tp = mesh.shape['tp']
    swap = [(i, num_tp - 1 - i) for i in range(num_tp)]

    def local_step(x_in, grad_y, w_query, w_key, w_value, w_out, w_up, b_up, w_down, ln_scale, q_scale, k_scale):
        num_img, num_tok, depth = x_in.shape
        total = num_img * num_tok
        width = w_query.shape[1]
        x2 = x_in.reshape(total, depth)
        gy2 = grad_y.reshape(total, depth)
        tp_idx = lax.axis_index('tp')

        w_qkv = gather_rows(jnp.concatenate([w_query, w_key, w_value], axis=1))
        wo = gather_cols(w_out)
        wu = gather_rows(w_up)
        wd = gather_cols(w_down)

        unit, _ = norm_parts(x2.astype(fp32))
        normed = (unit * ln_scale).astype(bf16)
        b_down_part = jnp.sum(gy2, axis=0, dtype=fp32)
        normed, b_down_part = lax.optimization_barrier((normed, b_down_part))

        qkv = dot_nn(normed, w_qkv).astype(bf16)
        d_attn = dot_nt(after(gy2, qkv), wo).astype(bf16)
        attn_out, d_qkv, dgq, dgk = attention(qkv, d_attn, q_scale, k_scale, num_img)
        gw_out = dot_tn(attn_out, gy2)
        gw_qkv = dot_tn(normed, after(d_qkv, gw_out))

        act_out, d_hid, db_part = mlp(after(normed, gw_qkv), gy2, wu, wd, b_up, 512, 1024, 256)

        rows = total // CHUNKS
        half = rows // num_tp
        mine = tp_idx * half
        theirs = (num_tp - 1) * half - mine

        def d_normed_of(chunk, hid):
            part = slice(chunk * rows, (chunk + 1) * rows)
            return dot_nt(hid[part], wu) + dot_nt(d_qkv[part], w_qkv)

        def exchange(d_norm):
            return lax.ppermute(lax.dynamic_slice_in_dim(d_norm, theirs, half), 'tp', swap)

        def finish(chunk, d_norm, other):
            own = lax.dynamic_slice_in_dim(d_norm, mine, half)
            cot = (own + other).astype(bf16).astype(fp32)
            begin = chunk * rows + mine
            x_unit, x_inv = norm_parts(lax.dynamic_slice_in_dim(x2, begin, half).astype(fp32))
            d_x = norm_back(x_unit, x_inv, ln_scale, cot)
            g_x = (lax.dynamic_slice_in_dim(gy2, begin, half).astype(fp32) + d_x).astype(bf16)
            return g_x, jnp.sum(cot * x_unit, axis=0)

        dn0 = d_normed_of(0, d_hid)
        got0 = exchange(dn0)
        dn1 = d_normed_of(1, after(d_hid, dn0))
        got1 = exchange(dn1)
        gw_down = dot_tn(after(act_out, dn1), gy2)
        dn2 = d_normed_of(2, after(d_hid, gw_down))
        got2 = exchange(dn2)
        dn3 = d_normed_of(3, after(d_hid, dn2))
        got3 = exchange(dn3)
        gx0, ls0 = finish(0, dn0, after(got0, dn3))
        gx1, ls1 = finish(1, dn1, after(got1, dn3))
        gw_up = dot_tn(normed, after(d_hid, dn3, gx0, gx1))
        gx2, ls2 = finish(2, dn2, after(got2, gw_up))
        gx3, ls3 = finish(3, dn3, after(got3, gw_up))

        own_parts = (gx0, gx1, gx2, gx3)
        back_parts = []
        for piece in own_parts:
            back_parts.append(lax.ppermute(piece, 'tp', swap))
        own_parts, back_parts = lax.optimization_barrier((own_parts, tuple(back_parts)))
        pieces = []
        for own, back in zip(own_parts, back_parts):
            pieces += [jnp.where(tp_idx == 0, own, back), jnp.where(tp_idx == 0, back, own)]
        grad_x = jnp.concatenate(pieces, axis=0)

        first = (tp_idx == 0).astype(fp32)
        b_up_slots = jnp.zeros((num_tp, b_up.shape[0]), fp32)
        b_up_slots = lax.dynamic_update_slice_in_dim(b_up_slots, jnp.sum(db_part, axis=0, keepdims=True), tp_idx, 0)
        small = lax.psum(jnp.concatenate([b_up_slots.reshape(-1), b_down_part * first, ls0 + ls1 + ls2 + ls3,
                                          jnp.sum(dgq, axis=0), jnp.sum(dgk, axis=0)]), ('tp', 'fsdp'))
        ends = [num_tp * b_up.shape[0], depth, depth, q_scale.shape[0], k_scale.shape[0]]
        spans, at = [], 0
        for size in ends:
            spans.append(small[at:at + size])
            at += size
        g_b_up = lax.dynamic_slice_in_dim(spans[0], tp_idx * b_up.shape[0], b_up.shape[0])

        s_out = scatter_cols(gw_out)
        s_qkv = scatter_rows(gw_qkv)
        s_down = scatter_cols(gw_down)
        s_up = scatter_rows(gw_up)
        return (grad_x.reshape(x_in.shape), s_qkv[:, :width], s_qkv[:, width:2 * width], s_qkv[:, 2 * width:],
                s_out, s_up, g_b_up, s_down, spans[1], spans[2], spans[3], spans[4])

    return jax.shard_map(local_step, mesh=mesh, in_specs=in_specs, out_specs=out_specs, check_vma=False)
```

time: 2210 us -> 1450 us (0.66)
  blocking collectives: 814 us -> 188 us
  matrix products: 1030 us -> 509 us
  waiting for transfers between devices: 20.8 us -> 368 us
  Pallas kernels: 0 us -> 234 us
  other arithmetic: 209 us -> 98.4 us
  local copies, waits for them, and re-layouts: 116 us -> 20.3 us
    psum x3 -> x1, blocking collectives: 814 us -> 188 us  [local_step(): lax.psum(jnp.concatenate([b_up_slots.reshape(-1), b_down_part * first, ls...]
    dot_general x22 -> x14, matrix products: 1030 us -> 509 us  [the longest x4 246 us: dot_tn(): lax.dot_general(a, b, (((0,), (0,)), ((), ())), preferred_element_type=fp32)]
    ppermute x0 -> x8, waiting for transfers between devices: none -> 327 us  [the longest x4 327 us: exchange(): lax.ppermute(lax.dynamic_slice_in_dim(d_norm, theirs, half), 'tp', swap)]
    pallas_call x0 -> x2, Pallas kernels: none -> 234 us  [the longest x1 177 us: mlp(): pl.pallas_call(functools.partial(mlp_kernel, sub), grid=(width // cols, t...]
    reduce_sum x10, other arithmetic: 146 us -> 42.5 us  [the longest x2 16 us: finish(): return (g_x, jnp.sum(cot * x_unit, axis=0))]
    convert_element_type x4 -> x0, local copies, waits for them, and re-layouts: 79.3 us -> none  [the longest x2 40.1 us: local_step(): kn_f, k_pull = jax.vjp(scaled_norm, k_proj.astype(fp32), k_scale)]
    unnamed x1 -> x14, other arithmetic: 0.01 us -> 25 us
    reshape x2 -> x0, local copies, waits for them, and re-layouts: 24 us -> none  [the longest x1 12.3 us: local_step(): d_attn_heads = d_attn.reshape(num_img, num_tok, num_heads, head_dim)]
  transfers between devices with their start and end apart: 12 -> 16, of which waited for: 1 -> 5; matrix products, arithmetic and copies ran while one was open for 61% -> 43% of each run, Pallas kernels for 0% -> 16%
where the time goes in v1:
time: 1450 us; the launch traced here: 1440 us
  matrix products  509 us (35%)
  waiting for transfers between devices  368 us (25%)
  Pallas kernels  234 us (16%)
  blocking collectives  188 us (13%)
  other arithmetic  98.4 us (7%)
  local copies, waits for them, and re-layouts  20.3 us (1%)
  between operations  15.1 us (1%)
    ppermute x4, waiting for transfers between devices, exchange(): lax.ppermute(lax.dynamic_slice_in_dim(d_norm, theirs, half), 'tp', swap)  327 us
    dot_general x4, matrix products, dot_tn(): lax.dot_general(a, b, (((0,), (0,)), ((), ())), preferred_element_type=fp32)  246 us
    dot_general x9, matrix products, dot_nt(): lax.dot_general(a, b, (((1,), (1,)), ((), ())), preferred_element_type=fp32)  203 us
    psum x1, blocking collectives, local_step(): lax.psum(jnp.concatenate([b_up_slots.reshape(-1), b_down_part * first, ls...  188 us
    pallas_call x1, Pallas kernels, mlp(): pl.pallas_call(functools.partial(mlp_kernel, sub), grid=(width // cols, t...  177 us
    dot_general x1, matrix products, dot_nn(): lax.dot_general(a, b, (((1,), (0,)), ((), ())), preferred_element_type=fp32)  60.2 us
    pallas_call x1, Pallas kernels, attention(): pl.pallas_call(functools.partial(attn_kernel, heads, dim), grid=(num_img,...  57.7 us
    all_gather x1, waiting for transfers between devices, local_step(): w_qkv = gather_rows(jnp.concatenate([w_query, w_key, w_value], axis=1))  38.7 us
  transfers between devices with their start and end apart: 16, of which 5 were waited for; matrix products, arithmetic and copies ran while one was open for 43% of the time, Pallas kernels for 16%

profile of v1, /device:TPU:0, one launch (start us, length us, event | category | flops | bytes accessed | tf_op | source)
XLA Modules:
  0.0 1442.6 jit_solution(11774428526444591449)
XLA Ops:
  32.8 10.0 multiply_convert_fusion.h_ref
  42.8 38.7 %all-gather.5.cloned.1.call-done = bf16[2048,3072]{1,0:T(8,128)(2,1)} async-done(((bf16[256,3072]{1,0:T(8,128)(2,1)}), bf16[2048,3072]{1,0:T(8,128)(2,1)}) %all-gather.5.cloned.1.call-update) | async-done | bytes 12582928 | tf_op jit(solution)/shard_map/all_gather | solution.py:166
  81.5 60.2 %convolution_convert_fusion.q_ref.k_ref.v_ref = bf16[4096,3072]{1,0:T(8,128)(2,1)} fusion(bf16[4096,2048]{1,0:T(8,128)(2,1)} %multiply_convert_fusion.h_ref, bf16[2048,3072]{1,0:T(8,128)(2,1)} %all-gather.5.cloned.1.call-done), kind=kOutput, calls=%fused_computation.6 | convolution fusion | flops 51552190464 | bytes 54525952 | tf_op jit(solution)/shard_map/dot_general | solution.py:16
  141.7 23.7 %convolution_convert_fusion.1.do_ref = bf16[4096,1024]{1,0:T(8,128)(2,1)} fusion(bf16[4096,2048]{1,0:T(8,128)(2,1)} %bitcast.42, bf16[1024,2048]{1,0:T(8,128)(2,1)} %all-gather.7.cloned.1.call-done), kind=kOutput, calls=%fused_computation.15 | convolution fusion | flops 17184063488 | bytes 29360128 | tf_op jit(solution)/shard_map/dot_general | solution.py:20
  165.4 57.7 %attn.1 = (bf16[4096,1024]{1,0:T(8,128)(2,1)}, bf16[4096,3072]{1,0:T(8,128)(2,1)}, f32[8,256]{1,0:T(8,128)}, f32[8,256]{1,0:T(8,128)}) custom-call(bf16[4096,3072]{1,0:T(8,128)(2,1)} %convolution_convert_fusion.q_ref.k_ref.v_ref, bf16[4096,3072]{1,0:T(8,128)(2,1)} %convolution_convert_fusion.q_ref.k_ref.v_ref, ...), custom_call_target="tpu_custom_call" | custom-call | flops 64424509440 | bytes 67108864 | tf_op jit(solution)/shard_map/attn/pallas_call | solution.py:87
  223.0 24.2 %fusion.86 = f32[1024,2048]{1,0:T(8,128)} fusion(bf16[4096,1024]{1,0:T(8,128)(2,1)} %get-tuple-element.44, bf16[4096,2048]{1,0:T(8,128)(2,1)} %bitcast.43), kind=kOutput, calls=%fused_computation.140 | convolution fusion | flops 17179869184 | bytes 33554432 | tf_op jit(solution)/shard_map/dot_general | solution.py:24
  247.3 62.5 %fusion.87 = f32[2048,3072]{1,0:T(8,128)} fusion(bf16[4096,2048]{1,0:T(8,128)(2,1)} %multiply_convert_fusion.h_ref, bf16[4096,3072]{1,0:T(8,128)(2,1)} %get-tuple-element.45), kind=kOutput, calls=%fused_computation.141 | convolution fusion | flops 51539607552 | bytes 67108864 | tf_op jit(solution)/shard_map/dot_general | solution.py:24
  310.5 20.1 %fusion.14 = f32[1024,2048]{1,0:T(8,128)} fusion(bf16[2048,3072]{1,0:T(8,128)(2,1)} %all-gather.5.cloned.1.call-done, bf16[4096,3072]{1,0:T(8,128)(2,1)} %get-tuple-element.45), kind=kOutput, calls=%fused_computation.20 | convolution fusion | flops 12884901888 | bytes 27262976 | tf_op jit(solution)/shard_map/dot_general | solution.py:20
  330.6 21.3 %fusion.16 = f32[1024,2048]{1,0:T(8,128)} fusion(bf16[2048,3072]{1,0:T(8,128)(2,1)} %all-gather.5.cloned.1.call-done, bf16[4096,3072]{1,0:T(8,128)(2,1)} %get-tuple-element.45), kind=kOutput, calls=%fused_computation.22 | convolution fusion | flops 12884901888 | bytes 27262976 | tf_op jit(solution)/shard_map/dot_general | solution.py:20
  351.8 176.7 %mlp.1 = (bf16[4096,4096]{1,0:T(8,128)(2,1)}, bf16[4096,4096]{1,0:T(8,128)(2,1)}, f32[8,4096]{1,0:T(8,128)}) custom-call(bf16[4096,2048]{1,0:T(8,128)(2,1)} %multiply_convert_fusion.h_ref, bf16[4096,2048]{1,0:T(8,128)(2,1)} %bitcast.44, bf16[2048,4096]{1,0:T(8,128)(2,1)} %all-gather.9.cloned.1.call-done.wu_ref, ...), custom_call_target="tpu_custom_call" | custom-call | flops 137438953472 | bytes 268435456 | tf_op jit(solution)/shard_map/mlp/pallas_call | solution.py:125
  528.6 25.2 %fusion.42 = f32[1024,2048]{1,0:T(8,128)} fusion(f32[1024,2048]{1,0:T(8,128)} %fusion.16, bf16[2048,4096]{1,0:T(8,128)(2,1)} %all-gather.9.cloned.1.call-done.wu_ref, bf16[4096,4096]{1,0:T(8,128)(2,1)} %get-tuple-element.55), kind=kOutput, calls=%fused_computation.64 | convolution fusion | flops 17181966336 | bytes 41943040 | tf_op jit(solution)/shard_map/dot_general | solution.py:20
  553.8 24.2 %fusion.45 = f32[1024,2048]{1,0:T(8,128)} fusion(f32[1024,2048]{1,0:T(8,128)S(1)} %copy-done.7, bf16[2048,4096]{1,0:T(8,128)(2,1)} %all-gather.9.cloned.1.call-done.wu_ref, bf16[4096,4096]{1,0:T(8,128)(2,1)} %get-tuple-element.55), kind=kOutput, calls=%fused_computation.65 | convolution fusion | flops 17181966336 | bytes 41943040 | tf_op jit(solution)/shard_map/dot_general | solution.py:20
  578.0 79.6 %fusion.88 = f32[4096,2048]{1,0:T(8,128)} fusion(bf16[4096,4096]{1,0:T(8,128)(2,1)} %get-tuple-element.50, bf16[4096,2048]{1,0:T(8,128)(2,1)} %bitcast.45), kind=kOutput, calls=%fused_computation.142 | convolution fusion | flops 68719476736 | bytes 83886080 | tf_op jit(solution)/shard_map/dot_general | solution.py:24
  667.1 21.4 %fusion.10 = f32[1024,2048]{1,0:T(8,128)} fusion(bf16[2048,3072]{1,0:T(8,128)(2,1)} %all-gather.5.cloned.1.call-done, bf16[4096,3072]{1,0:T(8,128)(2,1)} %get-tuple-element.45), kind=kOutput, calls=%fused_computation.16 | convolution fusion | flops 12884901888 | bytes 27262976 | tf_op jit(solution)/shard_map/dot_general | solution.py:20
  688.5 17.3 %fusion.12 = f32[1024,2048]{1,0:T(8,128)} fusion(bf16[2048,3072]{1,0:T(8,128)(2,1)S(1)} %bitcast.58, bf16[4096,3072]{1,0:T(8,128)(2,1)} %get-tuple-element.45), kind=kOutput, calls=%fused_computation.18 | convolution fusion | flops 12884901888 | bytes 27262976 | tf_op jit(solution)/shard_map/dot_general | solution.py:20
  705.8 25.1 %fusion.48 = f32[1024,2048]{1,0:T(8,128)} fusion(f32[1024,2048]{1,0:T(8,128)} %fusion.12, bf16[2048,4096]{1,0:T(8,128)(2,1)} %all-gather.9.cloned.1.call-done.wu_ref, bf16[4096,4096]{1,0:T(8,128)(2,1)} %get-tuple-element.55), kind=kOutput, calls=%fused_computation.66 | convolution fusion | flops 17181966336 | bytes 41943040 | tf_op jit(solution)/shard_map/dot_general | solution.py:20
  738.3 25.0 %fusion.51 = f32[1024,2048]{1,0:T(8,128)} fusion(f32[1024,2048]{1,0:T(8,128)} %fusion.10, bf16[2048,4096]{1,0:T(8,128)(2,1)} %all-gather.9.cloned.1.call-done.wu_ref, bf16[4096,4096]{1,0:T(8,128)(2,1)} %get-tuple-element.55), kind=kOutput, calls=%fused_computation.67 | convolution fusion | flops 17181966336 | bytes 41943040 | tf_op jit(solution)/shard_map/dot_general | solution.py:20
  763.3 61.6 %collective-permute-done = f32[512,2048]{1,0:T(8,128)} collective-permute-done((f32[512,2048]{1,0:T(8,128)S(1)}, f32[512,2048]{1,0:T(8,128)}, u32[]{:S(2)}, u32[]{:S(2)}) %collective-permute-start) | collective-permute-done | bytes 4194336 | tf_op jit(solution)/shard_map/ppermute | solution.py:194
  825.0 89.3 %collective-permute-done.1 = f32[512,2048]{1,0:T(8,128)} collective-permute-done((f32[512,2048]{1,0:T(8,128)}, f32[512,2048]{1,0:T(8,128)}, u32[]{:S(2)}, u32[]{:S(2)}) %collective-permute-start.1) | collective-permute-done | bytes 4194336 | tf_op jit(solution)/shard_map/ppermute | solution.py:194
  914.3 9.6 fusion.75
  931.0 79.4 %fusion.89 = f32[2048,4096]{1,0:T(8,128)} fusion(bf16[4096,2048]{1,0:T(8,128)(2,1)} %multiply_convert_fusion.h_ref, bf16[4096,4096]{1,0:T(8,128)(2,1)} %get-tuple-element.55), kind=kOutput, calls=%fused_computation.143 | convolution fusion | flops 68719476736 | bytes 83886080 | tf_op jit(solution)/shard_map/dot_general | solution.py:24
  1020.6 86.0 %collective-permute-done.2 = f32[512,2048]{1,0:T(8,128)S(1)} collective-permute-done((f32[512,2048]{1,0:T(8,128)S(1)}, f32[512,2048]{1,0:T(8,128)S(1)}, u32[]{:S(2)}, u32[]{:S(2)}) %collective-permute-start.2) | collective-permute-done | bytes 4194336 | tf_op jit(solution)/shard_map/ppermute | solution.py:194
  1106.5 89.9 %collective-permute-done.3 = f32[512,2048]{1,0:T(8,128)S(1)} collective-permute-done((f32[512,2048]{1,0:T(8,128)S(1)}, f32[512,2048]{1,0:T(8,128)S(1)}, u32[]{:S(2)}, u32[]{:S(2)}) %collective-permute-start.3) | collective-permute-done | bytes 4194336 | tf_op jit(solution)/shard_map/ppermute | solution.py:194
  1212.6 188.5 %psum.7 = f32[12800]{0:T(1024)S(1)} all-reduce(f32[12800]{0:T(1024)S(1)} %constant_dynamic-update-slice_fusion.1), channel_id=1, replica_groups=mesh['tp'=2,'fsdp'=8] {'tp','fsdp'}, use_global_device_ids=true, to_apply=%region_29.30 | all-reduce | flops 12800 | bytes 102400 | tf_op jit(solution)/shard_map/psum | solution.py:233
  (124 shorter events, 110.5 us)
Async XLA Ops:
  7.2 74.3 %all-gather.5.cloned.1.call-start = ((), (), s32[]{:S(2)}) async-start(), calls=%async_computation.4 | async-start | bytes 14155776 | tf_op jit(solution)/shard_map/all_gather | solution.py:166
  9.9 131.8 %all-gather.7.cloned.1.call-start = ((), (), s32[]{:S(2)}) async-start(), calls=%async_computation.5 | async-start | bytes 4718592 | tf_op jit(solution)/shard_map/all_gather | solution.py:167
  10.6 341.2 %all-gather.9.cloned.1.call-start = ((), (), s32[]{:S(2)}) async-start(), calls=%async_computation.6 | async-start | bytes 18874368 | tf_op jit(solution)/shard_map/all_gather | solution.py:168
  11.3 340.5 %all-gather.11.cloned.1.call-start = ((), (), s32[]{:S(2)}) async-start(), calls=%async_computation.7 | async-start | bytes 18874368 | tf_op jit(solution)/shard_map/all_gather | solution.py:169
  11.9 1419.8 %reduce-scatter.5.cloned.1.call-start = ((), (), s32[]{:S(2)}) async-start(), calls=%async_computation.8 | async-start | bytes 28311552 | tf_op jit(solution)/shard_map/reduce_scatter | solution.py:243
  309.8 1125.5 %reduce-scatter.7.cloned.1.call-start = ((), (), s32[]{:S(2)}) async-start(), calls=%async_computation.9 | async-start | bytes 9437184 | tf_op jit(solution)/shard_map/reduce_scatter | solution.py:242
  310.4 1124.9 %reduce-scatter.11.cloned.1.call-start = ((), (), s32[]{:S(2)}) async-start(), calls=%async_computation.11 | async-start | bytes 37748736 | tf_op jit(solution)/shard_map/reduce_scatter | solution.py:244
  528.6 25.2 %copy-start.7 = (f32[1024,2048]{1,0:T(8,128)S(1)}, f32[1024,2048]{1,0:T(8,128)}, u32[]{:S(2)}) copy-start(f32[1024,2048]{1,0:T(8,128)} %fusion.14) | copy-start | bytes 25165828
  657.6 777.8 %reduce-scatter.9.cloned.1.call-start = ((), (), s32[]{:S(2)}) async-start(), calls=%async_computation.10 | async-start | bytes 37748736 | tf_op jit(solution)/shard_map/reduce_scatter | solution.py:245
  660.5 28.0 %slice-start.4 = ((s8[12582912]{0:T(1024)(128)(4,1)}), s8[4194304]{0:T(1024)(128)(4,1)S(1)}, s32[]{:S(2)}) async-start(s8[12582912]{0:T(1024)(128)(4,1)} %bitcast.57), calls=%async_computation.16 | async-start | bytes 8388608
  667.0 21.4 %slice-start.5 = ((s8[12582912]{0:T(1024)(128)(4,1)}), s8[4194304]{0:T(1024)(128)(4,1)S(1)}, s32[]{:S(2)}) async-start(s8[12582912]{0:T(1024)(128)(4,1)} %bitcast.57), calls=%async_computation.17 | async-start | bytes 8388608
  688.5 42.4 %slice-start = ((s8[8388608]{0:T(1024)(128)(4,1)}), s8[4194304]{0:T(1024)(128)(4,1)S(1)}, s32[]{:S(2)}) async-start(s8[8388608]{0:T(1024)(128)(4,1)} %bitcast.48), calls=%async_computation.12 | async-start | bytes 8388608
  705.8 25.1 %slice-start.1 = ((s8[8388608]{0:T(1024)(128)(4,1)}), s8[4194304]{0:T(1024)(128)(4,1)S(1)}, s32[]{:S(2)}) async-start(s8[8388608]{0:T(1024)(128)(4,1)} %bitcast.48), calls=%async_computation.13 | async-start | bytes 8388608
  731.4 93.6 %collective-permute-start = (f32[512,2048]{1,0:T(8,128)S(1)}, f32[512,2048]{1,0:T(8,128)}, u32[]{:S(2)}, u32[]{:S(2)}) collective-permute-start(f32[512,2048]{1,0:T(8,128)S(1)} %constant_dynamic-slice_fusion.3), channel_id=1, source_target_pairs={{0,8},{8,0},{1,9},{9,1},{2,10},{10,2},{3,11},{11,3},{4,12},{12,4},... | collective-permute-start | bytes 12582920 | tf_op jit(solution)/shard_map/ppermute | solution.py:194
  737.4 176.9 %copy-start.2 = (f32[2048]{0:T(1024)S(1)}, f32[2048]{0:T(1024)}, u32[]{:S(2)}) copy-start(f32[2048]{0:T(1024)} %param.21) | copy-start | bytes 24580
  737.4 176.9 %collective-permute-start.1 = (f32[512,2048]{1,0:T(8,128)}, f32[512,2048]{1,0:T(8,128)}, u32[]{:S(2)}, u32[]{:S(2)}) collective-permute-start(f32[512,2048]{1,0:T(8,128)} %constant_dynamic-slice_fusion.2), channel_id=1, source_target_pairs={{0,8},{8,0},{1,9},{9,1},{2,10},{10,2},{3,11},{11,3},{4,12},{12,4},... | collective-permute-start | bytes 12582920 | tf_op jit(solution)/shard_map/ppermute | solution.py:194
  1010.4 186.0 %slice-start.2 = ((s8[8388608]{0:T(1024)(128)(4,1)}), s8[4194304]{0:T(1024)(128)(4,1)S(1)}, s32[]{:S(2)}) async-start(s8[8388608]{0:T(1024)(128)(4,1)} %bitcast.50), calls=%async_computation.14 | async-start | bytes 8388608
  1013.1 183.4 %slice-start.3 = ((s8[8388608]{0:T(1024)(128)(4,1)}), s8[4194304]{0:T(1024)(128)(4,1)S(1)}, s32[]{:S(2)}) async-start(s8[8388608]{0:T(1024)(128)(4,1)} %bitcast.50), calls=%async_computation.15 | async-start | bytes 8388608
  1013.1 93.5 %collective-permute-start.2 = (f32[512,2048]{1,0:T(8,128)S(1)}, f32[512,2048]{1,0:T(8,128)S(1)}, u32[]{:S(2)}, u32[]{:S(2)}) collective-permute-start(f32[512,2048]{1,0:T(8,128)S(1)} %constant_dynamic-slice_fusion.1), channel_id=1, source_target_pairs={{0,8},{8,0},{1,9},{9,1},{2,10},{10,2},{3,11},{11,3},{4,12},{12,4},... | collective-permute-start | bytes 12582920 | tf_op jit(solution)/shard_map/ppermute | solution.py:194
  1017.8 178.6 %collective-permute-start.3 = (f32[512,2048]{1,0:T(8,128)S(1)}, f32[512,2048]{1,0:T(8,128)S(1)}, u32[]{:S(2)}, u32[]{:S(2)}) collective-permute-start(f32[512,2048]{1,0:T(8,128)S(1)} %constant_dynamic-slice_fusion), channel_id=1, source_target_pairs={{0,8},{8,0},{1,9},{9,1},{2,10},{10,2},{3,11},{11,3},{4,12},{12,4},... | collective-permute-start | bytes 12582920 | tf_op jit(solution)/shard_map/ppermute | solution.py:194
  1018.5 384.4 %collective-permute-start.5 = (bf16[512,2048]{1,0:T(8,128)(2,1)S(1)}, bf16[512,2048]{1,0:T(8,128)(2,1)}, u32[]{:S(2)}, u32[]{:S(2)}) collective-permute-start(bf16[512,2048]{1,0:T(8,128)(2,1)S(1)} %get-tuple-element.60), channel_id=1, source_target_pairs={{0,8},{8,0},{1,9},{9,1},{2,10},{10,2},{3,11},{11,3},{4,12},{12,4},... | collective-permute-start | bytes 6291464 | tf_op jit(solution)/shard_map/ppermute | solution.py:223
  1019.9 383.0 %collective-permute-start.4 = (bf16[512,2048]{1,0:T(8,128)(2,1)}, bf16[512,2048]{1,0:T(8,128)(2,1)}, u32[]{:S(2)}, u32[]{:S(2)}) collective-permute-start(bf16[512,2048]{1,0:T(8,128)(2,1)} %get-tuple-element.58), channel_id=1, source_target_pairs={{0,8},{8,0},{1,9},{9,1},{2,10},{10,2},{3,11},{11,3},{4,12},{12,4},... | collective-permute-start | bytes 6291464 | tf_op jit(solution)/shard_map/ppermute | solution.py:223
  1210.2 192.7 %collective-permute-start.7 = (bf16[512,2048]{1,0:T(8,128)(2,1)}, bf16[512,2048]{1,0:T(8,128)(2,1)}, u32[]{:S(2)}, u32[]{:S(2)}) collective-permute-start(bf16[512,2048]{1,0:T(8,128)(2,1)} %get-tuple-element.64), channel_id=1, source_target_pairs={{0,8},{8,0},{1,9},{9,1},{2,10},{10,2},{3,11},{11,3},{4,12},{12,4},... | collective-permute-start | bytes 6291464 | tf_op jit(solution)/shard_map/ppermute | solution.py:223
  1211.8 191.2 %collective-permute-start.6 = (bf16[512,2048]{1,0:T(8,128)(2,1)}, bf16[512,2048]{1,0:T(8,128)(2,1)}, u32[]{:S(2)}, u32[]{:S(2)}) collective-permute-start(bf16[512,2048]{1,0:T(8,128)(2,1)} %get-tuple-element.62), channel_id=1, source_target_pairs={{0,8},{8,0},{1,9},{9,1},{2,10},{10,2},{3,11},{11,3},{4,12},{12,4},... | collective-permute-start | bytes 6291464 | tf_op jit(solution)/shard_map/ppermute | solution.py:223
  (7 other events, 77.2 us)
Sparse Core Ops, SparseCore 0:
  10.4 71.0 all-gather.4
  83.3 33.5 all-gather.6
  118.8 85.9 all-gather.8
  206.5 89.2 all-gather.10
  309.9 150.7 reduce-scatter.4
  464.5 65.6 reduce-scatter.6
  657.7 199.4 reduce-scatter.10
  1010.5 199.8 reduce-scatter.8

commit v2 on v1

--- a/solution.py
+++ b/solution.py
@@ -98,7 +98,9 @@
     )(qkv, qkv, qkv, d_attn, q_scale.reshape(1, dim), k_scale.reshape(1, dim))
 
 
-def mlp_kernel(sub, h_ref, gy_ref, wu_ref, wd_ref, b_ref, act_ref, dh_ref, db_ref):
+def mlp_kernel(sub, h_ref, gy_ref, wu_ref, wd_ref, b_ref, *refs):
+    act_ref, dh_ref, db_ref = refs[-3:]
+
     @pl.when(pl.program_id(1) == 0)
     def _():
         db_ref[...] = jnp.zeros_like(db_ref)
@@ -117,25 +119,30 @@
         db_ref[:, cols] += jnp.sum(d_hid.astype(fp32).reshape(-1, 8, sub), axis=0)
 
 
-def mlp(normed, grad_y, w_up, w_down, b_up, rows, cols, sub):
+def mlp(normed, grad_y, w_up, w_down, b_up, rows, cols, sub, part, parts, held):
     total, depth = normed.shape
     width = w_up.shape[1]
-    row_spec = pl.BlockSpec((rows, depth), lambda j, i: (i, 0))
-    out_spec = pl.BlockSpec((rows, cols), lambda j, i: (i, j))
+    steps = total // rows // parts
+    skip = part * steps
+    row_spec = pl.BlockSpec((rows, depth), lambda j, i: (i + skip, 0))
+    out_spec = pl.BlockSpec((rows, cols), lambda j, i: (i + skip, j))
     return pl.pallas_call(
         functools.partial(mlp_kernel, sub),
-        grid=(width // cols, total // rows),
+        grid=(width // cols, steps),
         in_specs=[row_spec, row_spec, pl.BlockSpec((depth, cols), lambda j, i: (0, j)),
-                  pl.BlockSpec((cols, depth), lambda j, i: (j, 0)), pl.BlockSpec((1, cols), lambda j, i: (0, j))],
+                  pl.BlockSpec((cols, depth), lambda j, i: (j, 0)), pl.BlockSpec((1, cols), lambda j, i: (0, j))]
+        + [pl.BlockSpec(memory_space=pl.ANY)] * len(held),
         out_specs=[out_spec, out_spec, pl.BlockSpec((8, cols), lambda j, i: (0, j))],
         out_shape=[jax.ShapeDtypeStruct((total, width), bf16), jax.ShapeDtypeStruct((total, width), bf16),
                    jax.ShapeDtypeStruct((8, width), fp32)],
+        input_output_aliases={5 + n: n for n in range(len(held))},
         compiler_params=pltpu.CompilerParams(dimension_semantics=("arbitrary", "arbitrary"),
                                              vmem_limit_bytes=60 * 2 ** 20),
-        cost_estimate=pl.CostEstimate(flops=4 * total * depth * width, bytes_accessed=16 * total * width,
-                                      transcendentals=2 * total * width),
+        cost_estimate=pl.CostEstimate(flops=4 * total * depth * width // parts,
+                                      bytes_accessed=16 * total * width // parts,
+                                      transcendentals=2 * total * width // parts),
         name="mlp",
-    )(normed, grad_y, w_up, w_down, b_up.reshape(1, width))
+    )(normed, grad_y, w_up, w_down, b_up.reshape(1, width), *held)
 
 
 def after(value, *earlier):
@@ -153,6 +160,7 @@
     scatter_rows = functools.partial(lax.psum_scatter, axis_name='fsdp', scatter_dimension=0, tiled=True)
     scatter_cols = functools.partial(lax.psum_scatter, axis_name='fsdp', scatter_dimension=1, tiled=True)
     num_tp = mesh.shape['tp']
+    num_fsdp = mesh.shape['fsdp']
     swap = [(i, num_tp - 1 - i) for i in range(num_tp)]
 
     def local_step(x_in, grad_y, w_query, w_key, w_value, w_out, w_up, b_up, w_down, ln_scale, q_scale, k_scale):
@@ -179,7 +187,8 @@
         gw_out = dot_tn(attn_out, gy2)
         gw_qkv = dot_tn(normed, after(d_qkv, gw_out))
 
-        act_out, d_hid, db_part = mlp(after(normed, gw_qkv), gy2, wu, wd, b_up, 512, 1024, 256)
+        def mlp_part(part, start, held):
+            return mlp(start, gy2, wu, wd, b_up, 512, 1024, 256, part, 2, held)
 
         rows = total // CHUNKS
         half = rows // num_tp
@@ -202,20 +211,22 @@
             g_x = (lax.dynamic_slice_in_dim(gy2, begin, half).astype(fp32) + d_x).astype(bf16)
             return g_x, jnp.sum(cot * x_unit, axis=0)
 
-        dn0 = d_normed_of(0, d_hid)
+        act_half, hid_half, db0 = mlp_part(0, after(normed, gw_qkv), ())
+        dn0 = d_normed_of(0, hid_half)
         got0 = exchange(dn0)
-        dn1 = d_normed_of(1, after(d_hid, dn0))
+        dn1 = d_normed_of(1, after(hid_half, dn0))
         got1 = exchange(dn1)
-        gw_down = dot_tn(after(act_out, dn1), gy2)
+        act_out, d_hid, db1 = mlp_part(1, after(normed, dn0, dn1), (act_half, hid_half))
+        gx0, ls0 = finish(0, dn0, after(got0, db1))
+        gw_down = dot_tn(act_out, after(gy2, gx0))
+        gx1, ls1 = finish(1, dn1, after(got1, gw_down))
         dn2 = d_normed_of(2, after(d_hid, gw_down))
         got2 = exchange(dn2)
         dn3 = d_normed_of(3, after(d_hid, dn2))
         got3 = exchange(dn3)
-        gx0, ls0 = finish(0, dn0, after(got0, dn3))
-        gx1, ls1 = finish(1, dn1, after(got1, dn3))
-        gw_up = dot_tn(normed, after(d_hid, dn3, gx0, gx1))
+        gw_up = dot_tn(normed, after(d_hid, dn3, gx1))
         gx2, ls2 = finish(2, dn2, after(got2, gw_up))
-        gx3, ls3 = finish(3, dn3, after(got3, gw_up))
+        gx3, ls3 = finish(3, dn3, after(got3, gx2))
 
         own_parts = (gx0, gx1, gx2, gx3)
         back_parts = []
@@ -229,9 +240,14 @@
 
         first = (tp_idx == 0).astype(fp32)
         b_up_slots = jnp.zeros((num_tp, b_up.shape[0]), fp32)
-        b_up_slots = lax.dynamic_update_slice_in_dim(b_up_slots, jnp.sum(db_part, axis=0, keepdims=True), tp_idx, 0)
-        small = lax.psum(jnp.concatenate([b_up_slots.reshape(-1), b_down_part * first, ls0 + ls1 + ls2 + ls3,
-                                          jnp.sum(dgq, axis=0), jnp.sum(dgk, axis=0)]), ('tp', 'fsdp'))
+        b_up_slots = lax.dynamic_update_slice_in_dim(b_up_slots, jnp.sum(db0 + db1, axis=0, keepdims=True), tp_idx, 0)
+        small = jnp.concatenate([b_up_slots.reshape(-1), b_down_part * first, ls0 + ls1 + ls2 + ls3,
+                                 jnp.sum(dgq, axis=0), jnp.sum(dgk, axis=0)])
+        bit = 1
+        while bit < num_fsdp:
+            small = small + lax.ppermute(small, 'fsdp', [(i, i ^ bit) for i in range(num_fsdp)])
+            bit *= 2
+        small = small + lax.ppermute(small, 'tp', swap)
         ends = [num_tp * b_up.shape[0], depth, depth, q_scale.shape[0], k_scale.shape[0]]
         spans, at = [], 0
         for size in ends:

time: 1450 us -> 1360 us (0.938)
  blocking collectives: 188 us -> 0 us
  waiting for transfers between devices: 368 us -> 440 us
    psum x1 -> x0, blocking collectives: 188 us -> none  [local_step(): lax.psum(jnp.concatenate([b_up_slots.reshape(-1), b_down_part * first, ls...]
    ppermute x0 -> x4, waiting for transfers between devices: none -> 164 us  [the longest x1 158 us: local_step(): small = small + lax.ppermute(small, 'tp', swap)]
    ppermute x4, waiting for transfers between devices: 327 us -> 234 us  [exchange(): lax.ppermute(lax.dynamic_slice_in_dim(d_norm, theirs, half), 'tp', swap)]
    pallas_call x1 -> x2, Pallas kernels: 177 us -> 184 us  [mlp(): pl.pallas_call(functools.partial(mlp_kernel, sub), grid=(width // cols, s...]
  transfers between devices with their start and end apart: 16 -> 20, of which waited for: 5 -> 8; matrix products, arithmetic and copies ran while one was open for 43% -> 47% of each run, Pallas kernels for 16% -> 18%
where the time goes in v2:
time: 1360 us; the launch traced here: 1350 us
  matrix products  514 us (38%)
  waiting for transfers between devices  440 us (32%)
  Pallas kernels  241 us (18%)
  other arithmetic  106 us (8%)
  local copies, waits for them, and re-layouts  20.2 us (1%)
  between operations  14.9 us (1%)
    dot_general x4, matrix products, dot_tn(): lax.dot_general(a, b, (((0,), (0,)), ((), ())), preferred_element_type=fp32)  246 us
    ppermute x4, waiting for transfers between devices, exchange(): lax.ppermute(lax.dynamic_slice_in_dim(d_norm, theirs, half), 'tp', swap)  234 us
    dot_general x9, matrix products, dot_nt(): lax.dot_general(a, b, (((1,), (1,)), ((), ())), preferred_element_type=fp32)  208 us
    pallas_call x2, Pallas kernels, mlp(): pl.pallas_call(functools.partial(mlp_kernel, sub), grid=(width // cols, s...  184 us
    ppermute x1, waiting for transfers between devices, local_step(): small = small + lax.ppermute(small, 'tp', swap)  158 us
    dot_general x1, matrix products, dot_nn(): lax.dot_general(a, b, (((1,), (0,)), ((), ())), preferred_element_type=fp32)  60.2 us
    pallas_call x1, Pallas kernels, attention(): pl.pallas_call(functools.partial(attn_kernel, heads, dim), grid=(num_img,...  57.7 us
    all_gather x1, waiting for transfers between devices, local_step(): w_qkv = gather_rows(jnp.concatenate([w_query, w_key, w_value], axis=1))  38.7 us
  transfers between devices with their start and end apart: 20, of which 8 were waited for; matrix products, arithmetic and copies ran while one was open for 47% of the time, Pallas kernels for 18%

profile of v2, /device:TPU:0, one launch (start us, length us, event | category | flops | bytes accessed | tf_op | source)
XLA Modules:
  0.0 1347.8 jit_solution(9083763275450273183)
XLA Ops:
  12.0 8.8 convert_reduce_fusion.1
  32.8 10.0 multiply_convert_fusion.h_ref
  42.8 38.7 %all-gather.5.cloned.1.call-done = bf16[2048,3072]{1,0:T(8,128)(2,1)} async-done(((bf16[256,3072]{1,0:T(8,128)(2,1)}), bf16[2048,3072]{1,0:T(8,128)(2,1)}) %all-gather.5.cloned.1.call-update) | async-done | bytes 12582928 | tf_op jit(solution)/shard_map/all_gather | solution.py:174
  81.5 60.2 %convolution_convert_fusion.q_ref.k_ref.v_ref = bf16[4096,3072]{1,0:T(8,128)(2,1)} fusion(bf16[4096,2048]{1,0:T(8,128)(2,1)} %multiply_convert_fusion.h_ref, bf16[2048,3072]{1,0:T(8,128)(2,1)} %all-gather.5.cloned.1.call-done), kind=kOutput, calls=%fused_computation.6 | convolution fusion | flops 51552190464 | bytes 54525952 | tf_op jit(solution)/shard_map/dot_general | solution.py:16
  141.7 23.9 %convolution_convert_fusion.1.do_ref = bf16[4096,1024]{1,0:T(8,128)(2,1)} fusion(bf16[4096,2048]{1,0:T(8,128)(2,1)} %bitcast.46, bf16[1024,2048]{1,0:T(8,128)(2,1)} %all-gather.7.cloned.1.call-done), kind=kOutput, calls=%fused_computation.15 | convolution fusion | flops 17184063488 | bytes 29360128 | tf_op jit(solution)/shard_map/dot_general | solution.py:20
  165.6 57.7 %attn.1 = (bf16[4096,1024]{1,0:T(8,128)(2,1)}, bf16[4096,3072]{1,0:T(8,128)(2,1)}, f32[8,256]{1,0:T(8,128)}, f32[8,256]{1,0:T(8,128)}) custom-call(bf16[4096,3072]{1,0:T(8,128)(2,1)} %convolution_convert_fusion.q_ref.k_ref.v_ref, bf16[4096,3072]{1,0:T(8,128)(2,1)} %convolution_convert_fusion.q_ref.k_ref.v_ref, ...), custom_call_target="tpu_custom_call" | custom-call | flops 64424509440 | bytes 67108864 | tf_op jit(solution)/shard_map/attn/pallas_call | solution.py:87
  223.3 24.1 %fusion.86 = f32[1024,2048]{1,0:T(8,128)} fusion(bf16[4096,1024]{1,0:T(8,128)(2,1)} %get-tuple-element.48, bf16[4096,2048]{1,0:T(8,128)(2,1)} %bitcast.47), kind=kOutput, calls=%fused_computation.141 | convolution fusion | flops 17179869184 | bytes 33554432 | tf_op jit(solution)/shard_map/dot_general | solution.py:24
  247.5 62.3 %fusion.87 = f32[2048,3072]{1,0:T(8,128)} fusion(bf16[4096,2048]{1,0:T(8,128)(2,1)} %multiply_convert_fusion.h_ref, bf16[4096,3072]{1,0:T(8,128)(2,1)} %get-tuple-element.49), kind=kOutput, calls=%fused_computation.142 | convolution fusion | flops 51539607552 | bytes 67108864 | tf_op jit(solution)/shard_map/dot_general | solution.py:24
  317.8 21.6 %fusion.14 = f32[1024,2048]{1,0:T(8,128)} fusion(bf16[2048,3072]{1,0:T(8,128)(2,1)} %all-gather.5.cloned.1.call-done, bf16[4096,3072]{1,0:T(8,128)(2,1)} %get-tuple-element.49), kind=kOutput, calls=%fused_computation.20 | convolution fusion | flops 12884901888 | bytes 27262976 | tf_op jit(solution)/shard_map/dot_general | solution.py:20
  339.4 19.3 %fusion.16 = f32[1024,2048]{1,0:T(8,128)} fusion(bf16[2048,3072]{1,0:T(8,128)(2,1)} %all-gather.5.cloned.1.call-done, bf16[4096,3072]{1,0:T(8,128)(2,1)} %get-tuple-element.49), kind=kOutput, calls=%fused_computation.22 | convolution fusion | flops 12884901888 | bytes 27262976 | tf_op jit(solution)/shard_map/dot_general | solution.py:20
  358.7 92.2 %mlp.2 = (bf16[4096,4096]{1,0:T(8,128)(2,1)}, bf16[4096,4096]{1,0:T(8,128)(2,1)}, f32[8,4096]{1,0:T(8,128)}) custom-call(bf16[4096,2048]{1,0:T(8,128)(2,1)} %multiply_convert_fusion.h_ref, bf16[4096,2048]{1,0:T(8,128)(2,1)} %bitcast.48, bf16[2048,4096]{1,0:T(8,128)(2,1)} %all-gather.9.cloned.1.call-done.wu_ref, ...), custom_call_target="tpu_custom_call" | custom-call | flops 68719476736 | bytes 134217728 | tf_op jit(solution)/shard_map/mlp/pallas_call | solution.py:129
  450.9 23.8 %fusion.42 = f32[1024,2048]{1,0:T(8,128)S(1)} fusion(f32[1024,2048]{1,0:T(8,128)} %fusion.16, bf16[2048,4096]{1,0:T(8,128)(2,1)} %all-gather.9.cloned.1.call-done.wu_ref, bf16[4096,4096]{1,0:T(8,128)(2,1)} %get-tuple-element.52.refs_1_), kind=kOutput, calls=%fused_computation.64 | convolution fusion | flops 17181966336 | bytes 41943040 | tf_op jit(solution)/shard_map/dot_general | solution.py:20
  474.8 28.2 %fusion.45 = f32[1024,2048]{1,0:T(8,128)} fusion(f32[1024,2048]{1,0:T(8,128)} %fusion.14, bf16[2048,4096]{1,0:T(8,128)(2,1)} %all-gather.9.cloned.1.call-done.wu_ref, bf16[4096,4096]{1,0:T(8,128)(2,1)} %get-tuple-element.52.refs_1_), kind=kOutput, calls=%fused_computation.65 | convolution fusion | flops 17181966336 | bytes 41943040 | tf_op jit(solution)/shard_map/dot_general | solution.py:20
  507.1 91.7 %mlp.3 = (bf16[4096,4096]{1,0:T(8,128)(2,1)}, bf16[4096,4096]{1,0:T(8,128)(2,1)}, f32[8,4096]{1,0:T(8,128)}) custom-call(bf16[4096,2048]{1,0:T(8,128)(2,1)} %multiply_convert_fusion.h_ref, bf16[4096,2048]{1,0:T(8,128)(2,1)} %bitcast.49, bf16[2048,4096]{1,0:T(8,128)(2,1)} %all-gather.9.cloned.1.call-done.wu_ref, ...), custom_call_target="tpu_custom_call", output_to_operand_aliasing={{0}: (5, {}), {1}: (6, {})} | custom-call | flops 68719476736 | bytes 134217728 | tf_op jit(solution)/shard_map/mlp/pallas_call | solution.py:129
  611.5 79.5 %fusion.88 = f32[4096,2048]{1,0:T(8,128)} fusion(bf16[4096,4096]{1,0:T(8,128)(2,1)} %get-tuple-element.57, bf16[4096,2048]{1,0:T(8,128)(2,1)} %bitcast.51), kind=kOutput, calls=%fused_computation.143 | convolution fusion | flops 68719476736 | bytes 83886080 | tf_op jit(solution)/shard_map/dot_general | solution.py:24
  691.1 19.6 %fusion.10 = f32[1024,2048]{1,0:T(8,128)} fusion(bf16[2048,3072]{1,0:T(8,128)(2,1)} %all-gather.5.cloned.1.call-done, bf16[4096,3072]{1,0:T(8,128)(2,1)} %get-tuple-element.49), kind=kOutput, calls=%fused_computation.16 | convolution fusion | flops 12884901888 | bytes 27262976 | tf_op jit(solution)/shard_map/dot_general | solution.py:20
  710.7 20.8 %fusion.12 = f32[1024,2048]{1,0:T(8,128)} fusion(bf16[2048,3072]{1,0:T(8,128)(2,1)} %all-gather.5.cloned.1.call-done, bf16[4096,3072]{1,0:T(8,128)(2,1)} %get-tuple-element.49), kind=kOutput, calls=%fused_computation.18 | convolution fusion | flops 12884901888 | bytes 27262976 | tf_op jit(solution)/shard_map/dot_general | solution.py:20
  735.1 26.0 %fusion.48 = f32[1024,2048]{1,0:T(8,128)} fusion(f32[1024,2048]{1,0:T(8,128)} %fusion.12, bf16[2048,4096]{1,0:T(8,128)(2,1)} %all-gather.9.cloned.1.call-done.wu_ref, bf16[4096,4096]{1,0:T(8,128)(2,1)} %get-tuple-element.63), kind=kOutput, calls=%fused_computation.66 | convolution fusion | flops 17181966336 | bytes 41943040 | tf_op jit(solution)/shard_map/dot_general | solution.py:20
  761.1 65.3 %collective-permute-done.1 = f32[512,2048]{1,0:T(8,128)S(1)} collective-permute-done((f32[512,2048]{1,0:T(8,128)}, f32[512,2048]{1,0:T(8,128)S(1)}, u32[]{:S(2)}, u32[]{:S(2)}) %collective-permute-start.1) | collective-permute-done | bytes 4194336 | tf_op jit(solution)/shard_map/ppermute | solution.py:203
  836.7 24.9 %fusion.51 = f32[1024,2048]{1,0:T(8,128)} fusion(f32[1024,2048]{1,0:T(8,128)} %fusion.10, bf16[2048,4096]{1,0:T(8,128)(2,1)} %all-gather.9.cloned.1.call-done.wu_ref, bf16[4096,4096]{1,0:T(8,128)(2,1)} %get-tuple-element.63), kind=kOutput, calls=%fused_computation.67 | convolution fusion | flops 17181966336 | bytes 41943040 | tf_op jit(solution)/shard_map/dot_general | solution.py:20
  861.7 80.0 %fusion.89 = f32[2048,4096]{1,0:T(8,128)} fusion(bf16[4096,2048]{1,0:T(8,128)(2,1)} %multiply_convert_fusion.h_ref, bf16[4096,4096]{1,0:T(8,128)(2,1)} %get-tuple-element.63), kind=kOutput, calls=%fused_computation.144 | convolution fusion | flops 68719476736 | bytes 83886080 | tf_op jit(solution)/shard_map/dot_general | solution.py:24
  949.9 88.0 %collective-permute-done.2 = f32[512,2048]{1,0:T(8,128)S(1)} collective-permute-done((f32[512,2048]{1,0:T(8,128)S(1)}, f32[512,2048]{1,0:T(8,128)S(1)}, u32[]{:S(2)}, u32[]{:S(2)}) %collective-permute-start.2) | collective-permute-done | bytes 4194336 | tf_op jit(solution)/shard_map/ppermute | solution.py:203
  1046.6 81.1 %collective-permute-done.3 = f32[512,2048]{1,0:T(8,128)S(1)} collective-permute-done((f32[512,2048]{1,0:T(8,128)S(1)}, f32[512,2048]{1,0:T(8,128)S(1)}, u32[]{:S(2)}, u32[]{:S(2)}) %collective-permute-start.3) | collective-permute-done | bytes 4194336 | tf_op jit(solution)/shard_map/ppermute | solution.py:203
  1148.7 157.7 %collective-permute-done.11 = f32[12800]{0:T(1024)S(1)} collective-permute-done((f32[12800]{0:T(1024)S(1)}, f32[12800]{0:T(1024)S(1)}, u32[]{:S(2)}, u32[]{:S(2)}) %collective-permute-start.11) | collective-permute-done | bytes 51232 | tf_op jit(solution)/shard_map/ppermute | solution.py:250
  (153 shorter events, 127.4 us)
Async XLA Ops:
  7.2 74.3 %all-gather.5.cloned.1.call-start = ((), (), s32[]{:S(2)}) async-start(), calls=%async_computation.4 | async-start | bytes 14155776 | tf_op jit(solution)/shard_map/all_gather | solution.py:174
  9.9 131.8 %all-gather.7.cloned.1.call-start = ((), (), s32[]{:S(2)}) async-start(), calls=%async_computation.5 | async-start | bytes 4718592 | tf_op jit(solution)/shard_map/all_gather | solution.py:175
  10.6 348.1 %all-gather.9.cloned.1.call-start = ((), (), s32[]{:S(2)}) async-start(), calls=%async_computation.6 | async-start | bytes 18874368 | tf_op jit(solution)/shard_map/all_gather | solution.py:176
  11.4 347.4 %all-gather.11.cloned.1.call-start = ((), (), s32[]{:S(2)}) async-start(), calls=%async_computation.7 | async-start | bytes 18874368 | tf_op jit(solution)/shard_map/all_gather | solution.py:177
  11.9 1325.2 %reduce-scatter.5.cloned.1.call-start = ((), (), s32[]{:S(2)}) async-start(), calls=%async_computation.8 | async-start | bytes 28311552 | tf_op jit(solution)/shard_map/reduce_scatter | solution.py:259
  309.8 1030.9 %reduce-scatter.7.cloned.1.call-start = ((), (), s32[]{:S(2)}) async-start(), calls=%async_computation.9 | async-start | bytes 9437184 | tf_op jit(solution)/shard_map/reduce_scatter | solution.py:258
  317.8 1022.9 %reduce-scatter.11.cloned.1.call-start = ((), (), s32[]{:S(2)}) async-start(), calls=%async_computation.11 | async-start | bytes 37748736 | tf_op jit(solution)/shard_map/reduce_scatter | solution.py:260
  505.3 93.5 %collective-permute-start = (f32[512,2048]{1,0:T(8,128)}, f32[512,2048]{1,0:T(8,128)}, u32[]{:S(2)}, u32[]{:S(2)}) collective-permute-start(f32[512,2048]{1,0:T(8,128)} %constant_dynamic-slice_fusion.3), channel_id=1, source_target_pairs={{0,8},{8,0},{1,9},{9,1},{2,10},{10,2},{3,11},{11,3},{4,12},{12,4},... | collective-permute-start | bytes 12582920 | tf_op jit(solution)/shard_map/ppermute | solution.py:203
  507.1 91.7 %copy-start.5 = (f32[2048]{0:T(1024)S(1)}, f32[2048]{0:T(1024)}, u32[]{:S(2)}) copy-start(f32[2048]{0:T(1024)} %param.21) | copy-start | bytes 24580
  507.1 91.7 %copy-start.12 = (f32[512]{0:T(512)S(1)}, f32[512]{0:T(512)}, u32[]{:S(2)}) copy-start(f32[512]{0:T(512)} %copy-done.11) | copy-start | bytes 6148
  507.1 91.7 %copy-start.13 = (f32[512]{0:T(512)S(1)}, f32[512]{0:T(512)}, u32[]{:S(2)}) copy-start(f32[512]{0:T(512)} %broadcast_multiply_fusion.9) | copy-start | bytes 6148
  507.1 91.7 %copy-start.15 = (f32[512]{0:T(512)S(1)}, f32[512]{0:T(512)}, u32[]{:S(2)}) copy-start(f32[512]{0:T(512)} %add_rsqrt_fusion.3) | copy-start | bytes 6148
  691.0 649.7 %reduce-scatter.9.cloned.1.call-start = ((), (), s32[]{:S(2)}) async-start(), calls=%async_computation.10 | async-start | bytes 37748736 | tf_op jit(solution)/shard_map/reduce_scatter | solution.py:261
  734.0 92.3 %collective-permute-start.1 = (f32[512,2048]{1,0:T(8,128)}, f32[512,2048]{1,0:T(8,128)S(1)}, u32[]{:S(2)}, u32[]{:S(2)}) collective-permute-start(f32[512,2048]{1,0:T(8,128)} %constant_dynamic-slice_fusion.2), channel_id=1, source_target_pairs={{0,8},{8,0},{1,9},{9,1},{2,10},{10,2},{3,11},{11,3},{4,12},{12,4},... | collective-permute-start | bytes 12582920 | tf_op jit(solution)/shard_map/ppermute | solution.py:203
  944.4 93.5 %collective-permute-start.2 = (f32[512,2048]{1,0:T(8,128)S(1)}, f32[512,2048]{1,0:T(8,128)S(1)}, u32[]{:S(2)}, u32[]{:S(2)}) collective-permute-start(f32[512,2048]{1,0:T(8,128)S(1)} %constant_dynamic-slice_fusion.1), channel_id=1, source_target_pairs={{0,8},{8,0},{1,9},{9,1},{2,10},{10,2},{3,11},{11,3},{4,12},{12,4},... | collective-permute-start | bytes 12582920 | tf_op jit(solution)/shard_map/ppermute | solution.py:203
  947.6 180.2 %collective-permute-start.3 = (f32[512,2048]{1,0:T(8,128)S(1)}, f32[512,2048]{1,0:T(8,128)S(1)}, u32[]{:S(2)}, u32[]{:S(2)}) collective-permute-start(f32[512,2048]{1,0:T(8,128)S(1)} %constant_dynamic-slice_fusion), channel_id=1, source_target_pairs={{0,8},{8,0},{1,9},{9,1},{2,10},{10,2},{3,11},{11,3},{4,12},{12,4},... | collective-permute-start | bytes 12582920 | tf_op jit(solution)/shard_map/ppermute | solution.py:203
  947.8 360.4 %collective-permute-start.4 = (bf16[512,2048]{1,0:T(8,128)(2,1)S(1)}, bf16[512,2048]{1,0:T(8,128)(2,1)}, u32[]{:S(2)}, u32[]{:S(2)}) collective-permute-start(bf16[512,2048]{1,0:T(8,128)(2,1)S(1)} %copy-done.1), channel_id=1, source_target_pairs={{0,8},{8,0},{1,9},{9,1},{2,10},{10,2},{3,11},{11,3},{4,12},{12,4},... | collective-permute-start | bytes 6291464 | tf_op jit(solution)/shard_map/ppermute | solution.py:234
  949.6 358.7 %collective-permute-start.5 = (bf16[512,2048]{1,0:T(8,128)(2,1)}, bf16[512,2048]{1,0:T(8,128)(2,1)}, u32[]{:S(2)}, u32[]{:S(2)}) collective-permute-start(bf16[512,2048]{1,0:T(8,128)(2,1)} %fusion.67), channel_id=1, source_target_pairs={{0,8},{8,0},{1,9},{9,1},{2,10},{10,2},{3,11},{11,3},{4,12},{12,4},... | collective-permute-start | bytes 6291464 | tf_op jit(solution)/shard_map/ppermute | solution.py:234
  1135.9 172.3 %collective-permute-start.7 = (bf16[512,2048]{1,0:T(8,128)(2,1)}, bf16[512,2048]{1,0:T(8,128)(2,1)}, u32[]{:S(2)}, u32[]{:S(2)}) collective-permute-start(bf16[512,2048]{1,0:T(8,128)(2,1)} %fusion.57), channel_id=1, source_target_pairs={{0,8},{8,0},{1,9},{9,1},{2,10},{10,2},{3,11},{11,3},{4,12},{12,4},... | collective-permute-start | bytes 6291464 | tf_op jit(solution)/shard_map/ppermute | solution.py:234
  1136.6 171.7 %collective-permute-start.6 = (bf16[512,2048]{1,0:T(8,128)(2,1)}, bf16[512,2048]{1,0:T(8,128)(2,1)}, u32[]{:S(2)}, u32[]{:S(2)}) collective-permute-start(bf16[512,2048]{1,0:T(8,128)(2,1)} %fusion.62), channel_id=1, source_target_pairs={{0,8},{8,0},{1,9},{9,1},{2,10},{10,2},{3,11},{11,3},{4,12},{12,4},... | collective-permute-start | bytes 6291464 | tf_op jit(solution)/shard_map/ppermute | solution.py:234
  1138.4 1.3 collective-permute-start.8
  1139.7 4.2 collective-permute-start.9
  1143.8 4.2 collective-permute-start.10
  1148.0 158.5 %collective-permute-start.11 = (f32[12800]{0:T(1024)S(1)}, f32[12800]{0:T(1024)S(1)}, u32[]{:S(2)}, u32[]{:S(2)}) collective-permute-start(f32[12800]{0:T(1024)S(1)} %add.185), channel_id=1, source_target_pairs={{0,8},{8,0},{1,9},{9,1},{2,10},{10,2},{3,11},{11,3},{4,12},{12,4},... | collective-permute-start | bytes 153608 | tf_op jit(solution)/shard_map/ppermute | solution.py:250
  (19 other events, 614.3 us)
Sparse Core Ops, SparseCore 0:
  10.4 71.0 all-gather.4
  83.3 33.5 all-gather.6
  118.8 85.9 all-gather.8
  206.5 89.2 all-gather.10
  309.9 150.7 reduce-scatter.4
  464.5 65.6 reduce-scatter.6
  691.2 199.9 reduce-scatter.10
  941.8 199.6 reduce-scatter.8
